TPU v7x, 512 devices: a whole 4x4x16 slice. The times are simulated.
512 devices in a mesh: cand: 16 (over y, z_hi, core), hid: 32 (over z_lo, x).
Axes of the slice: x: 4, y: 4, z: 16 (z_hi: 2, z_lo: 8; z = z_hi * 8 + z_lo), core: 2. Of those that a mesh axis runs over, the one named last changes fastest.
Arguments:
- tokens: bfloat16 [16, 256, 2048], P('cand', None, 'hid'), may hold values from -6 to 6
- cotangent: bfloat16 [16, 256, 2048], P('cand', None, 'hid'), may hold values from -6 to 6
- gate_weight: bfloat16 [2048, 8192], P('cand', 'hid'), may hold values from -0.125 to 0.125
- up_weight: bfloat16 [2048, 8192], P('cand', 'hid'), may hold values from -0.125 to 0.125
- down_weight: bfloat16 [8192, 2048], P('hid', 'cand'), may hold values from -0.125 to 0.125
- width_steps: int32 [16], P('cand'), may hold values from 1 to 8
- block_order: int32 [32], replicated, may hold values from 0 to 31, each once
Outputs:
- grad_tokens: float32 [16, 256, 2048], P('cand', None, 'hid')
- grad_gate: float32 [2048, 8192], P('cand', 'hid')
- grad_up: float32 [2048, 8192], P('cand', 'hid')
- grad_down: float32 [8192, 2048], P('hid', 'cand')
Inputs may be any that keep to these rules, and one draw needn't show every extreme that they name: Candidate c uses the first width_steps[c] * 1024 logical hidden units. `block_order`: names each of the 32 logical blocks once.
All inputs are finite; a program needn't handle non-finite values.
Results may differ from a plain program's by a relative error of at most 0.02.
Values may be sent and summed in bfloat16 or wider, within the bound.
No kernel may reach another device: no remote copies, remote signals or barrier semaphores. Data moves between devices by JAX's collectives and lax.ppermute only.
A program may use at most 64 MiB of HBM per device.

v0:
```python
import jax
import jax.numpy as jnp
from jax import lax
from jax.experimental import pallas as pl
from jax.experimental.pallas import tpu as pltpu
from jax.sharding import PartitionSpec as P

FF = 8192
TOK = 256
LANES = 128
BLK = 256
Y_GROUPS = [[4 * y + r for y in range(4)] for r in range(4)]
Z_GROUPS = [[8 * q + r for q in range(4)] for r in range(8)]


VMEM = pl.BlockSpec(memory_space=pltpu.VMEM)
SMEM = pl.BlockSpec(memory_space=pltpu.SMEM)
F32 = jnp.float32
BF16 = jnp.bfloat16


def swap(v, axis, offset):
    return lax.ppermute(v, axis, [(k, k ^ offset) for k in range(lax.axis_size(axis))])


def exchange(v, axis, groups):
    return lax.all_to_all(v, axis, 0, 0, axis_index_groups=groups, tiled=True)


def gather(v, axis, groups):
    return exchange(jnp.broadcast_to(v[None], (4, *v.shape)), axis, groups)


def total(v):
    return jnp.sum(v.astype(F32), axis=0)


def halves_mask(shape, parity):
    return (lax.broadcasted_iota(jnp.int32, shape, 1) < LANES // 2) == (parity == 0)


def forward_kernel(place, keep_ref, lo0, lo1, lo2, lo3, hi0, hi1, hi2, hi3, w0, w1, w2, w3,
                   own0, own1, away0, away1, dgu, tok, cot, hid):
    side, core, parity, quarter = place[0], place[1], place[2], place[3]
    mask = halves_mask((TOK, LANES), parity)
    pairs = ((lo0, lo1, 0, 0), (lo2, lo3, 1, 0), (hi0, hi1, 0, 1), (hi2, hi3, 1, 1))
    for even, odd, half, turn in pairs:
        chunk = (half ^ core) * 2 + (turn ^ side)
        for s, q in enumerate((0, 2, 1, 3)):
            lanes = pl.ds(pl.multiple_of((chunk * 4 + (quarter ^ q)) * LANES, LANES), LANES)
            e, f = even[s], odd[s]
            tok[:, lanes] = jnp.where(mask, e, f)
            cot[:, lanes] = jnp.where(mask, f, e)
    gate_up = jnp.zeros((TOK, 2 * BLK), F32)
    dhid = jnp.zeros((TOK, BLK), F32)
    for k, w in enumerate((w0, w1, w2, w3)):
        cols = slice(k * 512, (k + 1) * 512)
        wk = w[...].reshape(512, 3 * BLK)
        gate_up += jnp.dot(tok[:, cols], wk[:, : 2 * BLK], preferred_element_type=F32)
        dhid += jnp.dot(cot[:, cols], wk[:, 2 * BLK :], preferred_element_type=F32)
    keep = keep_ref[0]
    gate, up = gate_up[:, :BLK], gate_up[:, BLK:]
    sig = jax.nn.sigmoid(gate)
    act = keep * gate * sig
    dhid = keep * dhid
    hid[...] = (act * up).astype(BF16)
    dgu[:, BLK:] = (dhid * act).astype(BF16)
    dgu[:, :BLK] = (dhid * up * keep * sig * (1.0 + gate * (1.0 - sig))).astype(BF16)
    dims = (((0,), (0,)), ((), ()))
    for k, out in ((3, away1), (2, away0), (1, own1), (0, own0)):
        cols = slice(k * 512, (k + 1) * 512)
        gu = lax.dot_general(tok[:, cols], dgu[...], dims, preferred_element_type=F32)
        dn = lax.dot_general(cot[:, cols], hid[...], dims, preferred_element_type=F32)
        out[:, :, : 2 * BLK] = gu.astype(BF16).reshape(4, 128, 2 * BLK)
        out[:, :, 2 * BLK :] = dn.astype(BF16).reshape(4, 128, BLK)


def shard_kernel(gate, up, down, out):
    out[:, :BLK] = gate[...]
    out[:, BLK : 2 * BLK] = up[...]
    turned = down[...].T
    out[:64, 2 * BLK :] = turned[64:]
    out[64:, 2 * BLK :] = turned[:64]


def token_grads_kernel(place, dgu, w0, w1, w2, w3, out):
    side, core, parity = place[0], place[1], place[2]
    mask = halves_mask((TOK // 2, LANES), parity)
    dims = (((1,), (1,)), ((), ()))
    for k, w in enumerate((w0, w1, w2, w3)):
        wk = w[...].reshape(512, 3 * BLK)[:, : 2 * BLK]
        part = lax.dot_general(dgu[...], wk, dims, preferred_element_type=F32)
        x, turn = 2 * (k // 2 ^ core), k % 2 ^ side
        for q in range(4):
            block = part[:, q * LANES : (q + 1) * LANES]
            top = block[: TOK // 2]
            low = pltpu.roll(block[TOK // 2 :], LANES // 2, 1)
            out[x, turn, q] = jnp.where(mask, top, low).astype(BF16)
            out[x + 1, turn, q] = jnp.where(mask, low, top).astype(BF16)


def call(kernel, outs, n_smem, n_in, scratch, mib):
    run = pl.pallas_call(
        kernel,
        out_shape=outs,
        in_specs=[SMEM] * n_smem + [VMEM] * n_in,
        out_specs=[VMEM] * len(outs),
        scratch_shapes=list(scratch),
        compiler_params=pltpu.CompilerParams(vmem_limit_bytes=mib * 1024 * 1024),
    )
    return run


def sds(*shape, dtype=BF16):
    return jax.ShapeDtypeStruct(shape, dtype)


def step(tokens, cotangent, gate_weight, up_weight, down_weight, width_steps, block_order):
    c, h = lax.axis_index("cand"), lax.axis_index("hid")
    parity = h % 2
    place = jnp.stack([(h // 4 ^ c // 2) % 2, (c ^ h // 2) % 2, parity, h // 8]).astype(jnp.int32)
    places = jnp.arange(block_order.shape[0], dtype=jnp.int32)
    logical = jnp.sum(jnp.where(places == h, block_order, 0))
    keep = (logical * BLK < width_steps[0] * (FF // 8)).astype(F32).reshape(1)

    t, u = tokens[0], cotangent[0]
    first, second = jnp.where(parity == 0, t, u), jnp.where(parity == 0, u, t)
    piece = jnp.concatenate([first, second], axis=1)[None]
    (shard,) = call(shard_kernel, [sds(128, 3 * BLK)], 0, 3, [], 4)(
        gate_weight, up_weight, down_weight
    )

    pieces = jnp.concatenate([piece, swap(piece, "hid", 16)], axis=0)
    far = swap(shard, "cand", 2)
    w_own = gather(shard, "cand", Y_GROUPS)
    pieces = jnp.concatenate([pieces, swap(pieces, "hid", 8)], axis=0)
    pieces, place, keep = lax.optimization_barrier((pieces, place, keep))
    others = swap(pieces, "hid", 4)
    los = [pieces] + [swap(pieces, "hid", b) for b in (1, 2, 3)]
    his = [others] + [swap(others, "hid", b) for b in (1, 2, 3)]
    w_far = gather(far, "cand", Y_GROUPS)
    weights = [w_own, w_far, swap(w_own, "cand", 1), swap(w_far, "cand", 1)]

    grad = sds(4, 128, 3 * BLK)
    own0, own1, away0, away1, dgu = call(
        forward_kernel, [grad] * 4 + [sds(TOK, 2 * BLK)], 2, 12,
        [pltpu.VMEM((TOK, 2048), BF16)] * 2 + [pltpu.VMEM((TOK, BLK), BF16)], 12,
    )(place, keep, *los, *his, *weights)
    (parts,) = call(token_grads_kernel, [sds(4, 2, 4, 128, 128)], 1, 5, [], 8)(place, dgu, *weights)

    both1 = own1.astype(F32) + swap(away1, "cand", 1).astype(F32)
    total1 = total(exchange(both1.astype(BF16), "cand", Y_GROUPS))
    arrived0 = swap(away0, "cand", 1)
    both0 = (own0.astype(F32) + arrived0.astype(F32)).astype(BF16)
    grads = total(exchange(both0, "cand", Y_GROUPS))
    grads = grads + swap(total1.astype(BF16), "cand", 2).astype(F32)

    arrived = [swap(parts[b], "hid", b) for b in (1, 2, 3)]
    part = parts[0].astype(F32)
    for r in arrived:
        part = part + r.astype(F32)
    part = part[0] + swap(part[1].astype(BF16), "hid", 4).astype(F32)
    part = total(exchange(part.astype(BF16), "hid", Z_GROUPS))
    left, right = part[:, :64], part[:, 64:]
    top, low = jnp.where(parity == 0, left, right), jnp.where(parity == 0, right, left)
    grad_tokens = jnp.concatenate([top, low], axis=0)[None]

    grad_down = grads[:, 2 * BLK :]
    grad_down = jnp.concatenate([grad_down[64:], grad_down[:64]], axis=0).T
    return grad_tokens, grads[:, :BLK], grads[:, BLK : 2 * BLK], grad_down


def solution(mesh):
    in_specs = (
        P("cand", None, "hid"),
        P("cand", None, "hid"),
        P("cand", "hid"),
        P("cand", "hid"),
        P("hid", "cand"),
        P("cand"),
        P(),
    )
    out_specs = (P("cand", None, "hid"), P("cand", "hid"), P("cand", "hid"), P("hid", "cand"))
    return jax.shard_map(step, mesh=mesh, in_specs=in_specs, out_specs=out_specs, check_vma=False)
```

profile of v0, /device:TPU:72, one launch (start us, length us, event | category | flops | bytes accessed | tf_op | source)
XLA Modules:
  0.0 204.9 jit_solution(5160253701014070745)
XLA Ops:
  0.6 0.8 copy-done.4
  1.5 0.8 copy-done.5
  2.3 0.8 copy-done.6
  3.2 1.0 broadcast_in_dim.24
  4.2 5.0 %all-to-all-start = ((bf16[4,128,768]{2,1,0:T(8,128)(2,1)}), bf16[4,128,768]{2,1,0:T(8,128)(2,1)S(1)}, u32[]{:S(2)}, u32[]{:S(2)}) async-start(bf16[4,128,768]{2,1,0:T(8,128)(2,1)} %broadcast_in_dim.24), calls=%async_computation | async-start | bytes 1572864 | tf_op jit(solution)/shard_map/all_to_all | solution.py:27
  9.2 13.9 %collective-permute-start.9 = (bf16[128,768]{1,0:T(8,128)(2,1)S(1)}, bf16[128,768]{1,0:T(8,128)(2,1)S(1)}, u32[]{:S(2)}, u32[]{:S(2)}) collective-permute-start(bf16[128,768]{1,0:T(8,128)(2,1)S(1)} %shard_map.102), channel_id=1, source_target_pairs={{0,64},{32,96},{64,0},{96,32},{128,192},{160,224},{192,128},{224,1... | collective-permute-start | bytes 589832 | tf_op jit(solution)/shard_map/ppermute | solution.py:23
  23.5 11.8 %collective-permute-done.9 = bf16[128,768]{1,0:T(8,128)(2,1)S(1)} collective-permute-done((bf16[128,768]{1,0:T(8,128)(2,1)S(1)}, bf16[128,768]{1,0:T(8,128)(2,1)S(1)}, u32[]{:S(2)}, u32[]{:S(2)}) %collective-permute-start.9) | collective-permute-done | bytes 196640 | tf_op jit(solution)/shard_map/ppermute | solution.py:23
  35.3 1.0 broadcast_in_dim.25
  36.2 4.9 %all-to-all-start.1 = ((bf16[4,128,768]{2,1,0:T(8,128)(2,1)}), bf16[4,128,768]{2,1,0:T(8,128)(2,1)S(1)}, u32[]{:S(2)}, u32[]{:S(2)}) async-start(bf16[4,128,768]{2,1,0:T(8,128)(2,1)} %broadcast_in_dim.25), calls=%async_computation.1 | async-start | bytes 1572864 | tf_op jit(solution)/shard_map/all_to_all | solution.py:27
  41.3 11.7 %collective-permute-start = (bf16[1,256,128]{2,1,0:T(8,128)(2,1)S(1)}, bf16[1,256,128]{2,1,0:T(8,128)(2,1)S(1)}, u32[]{:S(2)}, u32[]{:S(2)}) collective-permute-start(bf16[1,256,128]{2,1,0:T(8,128)(2,1)S(1)} %maximum_bitcast_fusion.2), channel_id=1, source_target_pairs={{0,16},{1,17},{2,18},{3,19},{4,20},{5,21},{6,22},{7,23},{8,24},{9,... | collective-permute-start | bytes 196616 | tf_op jit(solution)/shard_map/ppermute | solution.py:23
  53.0 3.2 %collective-permute-done = bf16[1,256,128]{2,1,0:T(8,128)(2,1)S(1)} collective-permute-done((bf16[1,256,128]{2,1,0:T(8,128)(2,1)S(1)}, bf16[1,256,128]{2,1,0:T(8,128)(2,1)S(1)}, u32[]{:S(2)}, u32[]{:S(2)}) %collective-permute-start) | collective-permute-done | bytes 65568 | tf_op jit(solution)/shard_map/ppermute | solution.py:23
  56.2 1.9 collective-permute-start.1
  60.1 3.8 %collective-permute-done.1 = bf16[2,256,128]{2,1,0:T(8,128)(2,1)S(1)} collective-permute-done((bf16[2,256,128]{2,1,0:T(8,128)(2,1)S(1)}, bf16[2,256,128]{2,1,0:T(8,128)(2,1)S(1)}, u32[]{:S(2)}, u32[]{:S(2)}) %collective-permute-start.1) | collective-permute-done | bytes 131104 | tf_op jit(solution)/shard_map/ppermute | solution.py:23
  64.0 1.9 collective-permute-start.5
  65.9 1.9 collective-permute-start.10
  67.8 2.4 %collective-permute-start.11 = (bf16[4,128,768]{2,1,0:T(8,128)(2,1)S(1)}, bf16[4,128,768]{2,1,0:T(8,128)(2,1)S(1)}, u32[]{:S(2)}, u32[]{:S(2)}) collective-permute-start(bf16[4,128,768]{2,1,0:T(8,128)(2,1)S(1)} %all-to-all-done.1.w1), channel_id=1, source_target_pairs={{0,32},{32,0},{64,96},{96,64},{128,160},{160,128},{192,224},{224,1... | collective-permute-start | bytes 2359304 | tf_op jit(solution)/shard_map/ppermute | solution.py:23
  70.2 4.7 %collective-permute-start.4 = (bf16[4,256,128]{2,1,0:T(8,128)(2,1)S(1)}, bf16[4,256,128]{2,1,0:T(8,128)(2,1)S(1)}, u32[]{:S(2)}, u32[]{:S(2)}) collective-permute-start(bf16[4,256,128]{2,1,0:T(8,128)(2,1)S(1)} %pad_maximum_fusion.lo0), channel_id=1, source_target_pairs={{0,3},{1,2},{2,1},{3,0},{4,7},{5,6},{6,5},{7,4},{8,11},{9,10},{10,... | collective-permute-start | bytes 786440 | tf_op jit(solution)/shard_map/ppermute | solution.py:23
  74.9 2.7 %collective-permute-start.3 = (bf16[4,256,128]{2,1,0:T(8,128)(2,1)S(1)}, bf16[4,256,128]{2,1,0:T(8,128)(2,1)S(1)}, u32[]{:S(2)}, u32[]{:S(2)}) collective-permute-start(bf16[4,256,128]{2,1,0:T(8,128)(2,1)S(1)} %pad_maximum_fusion.lo0), channel_id=1, source_target_pairs={{0,2},{1,3},{2,0},{3,1},{4,6},{5,7},{6,4},{7,5},{8,10},{9,11},{10,... | collective-permute-start | bytes 786440 | tf_op jit(solution)/shard_map/ppermute | solution.py:23
  77.6 2.4 %collective-permute-start.2 = (bf16[4,256,128]{2,1,0:T(8,128)(2,1)S(1)}, bf16[4,256,128]{2,1,0:T(8,128)(2,1)S(1)}, u32[]{:S(2)}, u32[]{:S(2)}) collective-permute-start(bf16[4,256,128]{2,1,0:T(8,128)(2,1)S(1)} %pad_maximum_fusion.lo0), channel_id=1, source_target_pairs={{0,1},{1,0},{2,3},{3,2},{4,5},{5,4},{6,7},{7,6},{8,9},{9,8},{10,11... | collective-permute-start | bytes 786440 | tf_op jit(solution)/shard_map/ppermute | solution.py:23
  80.1 6.8 %collective-permute-done.4.lo3 = bf16[4,256,128]{2,1,0:T(8,128)(2,1)S(1)} collective-permute-done((bf16[4,256,128]{2,1,0:T(8,128)(2,1)S(1)}, bf16[4,256,128]{2,1,0:T(8,128)(2,1)S(1)}, u32[]{:S(2)}, u32[]{:S(2)}) %collective-permute-start.4) | collective-permute-done | bytes 262176 | tf_op jit(solution)/shard_map/ppermute | solution.py:23
  86.9 5.0 %collective-permute-start.8 = (bf16[4,256,128]{2,1,0:T(8,128)(2,1)S(1)}, bf16[4,256,128]{2,1,0:T(8,128)(2,1)S(1)}, u32[]{:S(2)}, u32[]{:S(2)}) collective-permute-start(bf16[4,256,128]{2,1,0:T(8,128)(2,1)S(1)} %collective-permute-done.5.hi0), channel_id=1, source_target_pairs={{0,3},{1,2},{2,1},{3,0},{4,7},{5,6},{6,5},{7,4},{8,11},{9,10},{10,... | collective-permute-start | bytes 786440 | tf_op jit(solution)/shard_map/ppermute | solution.py:23
  91.9 1.9 collective-permute-start.7
  93.8 2.9 %collective-permute-start.6 = (bf16[4,256,128]{2,1,0:T(8,128)(2,1)S(1)}, bf16[4,256,128]{2,1,0:T(8,128)(2,1)S(1)}, u32[]{:S(2)}, u32[]{:S(2)}) collective-permute-start(bf16[4,256,128]{2,1,0:T(8,128)(2,1)S(1)} %collective-permute-done.5.hi0), channel_id=1, source_target_pairs={{0,1},{1,0},{2,3},{3,2},{4,5},{5,4},{6,7},{7,6},{8,9},{9,8},{10,11... | collective-permute-start | bytes 786440 | tf_op jit(solution)/shard_map/ppermute | solution.py:23
  97.4 4.9 %collective-permute-done.8.hi3 = bf16[4,256,128]{2,1,0:T(8,128)(2,1)S(1)} collective-permute-done((bf16[4,256,128]{2,1,0:T(8,128)(2,1)S(1)}, bf16[4,256,128]{2,1,0:T(8,128)(2,1)S(1)}, u32[]{:S(2)}, u32[]{:S(2)}) %collective-permute-start.8) | collective-permute-done | bytes 262176 | tf_op jit(solution)/shard_map/ppermute | solution.py:23
  102.3 2.1 %collective-permute-done.7.hi2 = bf16[4,256,128]{2,1,0:T(8,128)(2,1)S(1)} collective-permute-done((bf16[4,256,128]{2,1,0:T(8,128)(2,1)S(1)}, bf16[4,256,128]{2,1,0:T(8,128)(2,1)S(1)}, u32[]{:S(2)}, u32[]{:S(2)}) %collective-permute-start.7) | collective-permute-done | bytes 262176 | tf_op jit(solution)/shard_map/ppermute | solution.py:23
  104.4 1.2 collective-permute-done.6.hi1
  105.6 0.9 copy-done.3
  106.6 4.2 %shard_map.103 = (bf16[4,128,768]{2,1,0:T(8,128)(2,1)S(1)}, bf16[4,128,768]{2,1,0:T(8,128)(2,1)S(1)}, bf16[4,128,768]{2,1,0:T(8,128)(2,1)}, bf16[4,128,768]{2,1,0:T(8,128)(2,1)}, bf16[256,512]{1,0:T(8,128)(2,1)S(1)}) custom-call(s32[4]{0:T(128)S(1)} %pad_add_fusion.place, f32[1]{0:T(128)} %bitcast.8.keep_ref, bf16[4,256,128]{2,1,0:T(8,128)(2,1)S(1)} %pad_maximum_fusion.lo0, ...), custom_call_target="tpu_custom_call" | custom-call | tf_op jit(solution)/shard_map/pallas_call | solution.py:145
  110.8 1.4 shard_map.104
  112.3 3.1 %collective-permute-start.12 = (bf16[2,4,128,128]{3,2,1,0:T(8,128)(2,1)S(1)}, bf16[2,4,128,128]{3,2,1,0:T(8,128)(2,1)S(1)}, u32[]{:S(2)}, u32[]{:S(2)}) collective-permute-start(bf16[2,4,128,128]{3,2,1,0:T(8,128)(2,1)S(1)} %get-tuple-element.28), channel_id=1, source_target_pairs={{0,1},{1,0},{2,3},{3,2},{4,5},{5,4},{6,7},{7,6},{8,9},{9,8},{10,11... | collective-permute-start | bytes 786440 | tf_op jit(solution)/shard_map/ppermute | solution.py:23
  115.3 3.7 %collective-permute-start.14 = (bf16[2,4,128,128]{3,2,1,0:T(8,128)(2,1)S(1)}, bf16[2,4,128,128]{3,2,1,0:T(8,128)(2,1)S(1)}, u32[]{:S(2)}, u32[]{:S(2)}) collective-permute-start(bf16[2,4,128,128]{3,2,1,0:T(8,128)(2,1)S(1)} %get-tuple-element.29), channel_id=1, source_target_pairs={{0,3},{1,2},{2,1},{3,0},{4,7},{5,6},{6,5},{7,4},{8,11},{9,10},{10,... | collective-permute-start | bytes 786440 | tf_op jit(solution)/shard_map/ppermute | solution.py:23
  119.0 3.4 %collective-permute-start.13 = (bf16[2,4,128,128]{3,2,1,0:T(8,128)(2,1)S(1)}, bf16[2,4,128,128]{3,2,1,0:T(8,128)(2,1)S(1)}, u32[]{:S(2)}, u32[]{:S(2)}) collective-permute-start(bf16[2,4,128,128]{3,2,1,0:T(8,128)(2,1)S(1)} %get-tuple-element.30), channel_id=1, source_target_pairs={{0,2},{1,3},{2,0},{3,1},{4,6},{5,7},{6,4},{7,5},{8,10},{9,11},{10,... | collective-permute-start | bytes 786440 | tf_op jit(solution)/shard_map/ppermute | solution.py:23
  122.4 2.1 %collective-permute-start.17 = (bf16[4,128,768]{2,1,0:T(8,128)(2,1)}, bf16[4,128,768]{2,1,0:T(8,128)(2,1)S(1)}, u32[]{:S(2)}, u32[]{:S(2)}) collective-permute-start(bf16[4,128,768]{2,1,0:T(8,128)(2,1)} %get-tuple-element.19), channel_id=1, source_target_pairs={{0,32},{32,0},{64,96},{96,64},{128,160},{160,128},{192,224},{224,1... | collective-permute-start | bytes 2359304 | tf_op jit(solution)/shard_map/ppermute | solution.py:23
  124.5 5.9 %collective-permute-done.14 = bf16[2,4,128,128]{3,2,1,0:T(8,128)(2,1)S(1)} collective-permute-done((bf16[2,4,128,128]{3,2,1,0:T(8,128)(2,1)S(1)}, bf16[2,4,128,128]{3,2,1,0:T(8,128)(2,1)S(1)}, u32[]{:S(2)}, u32[]{:S(2)}) %collective-permute-start.14) | collective-permute-done | bytes 262176 | tf_op jit(solution)/shard_map/ppermute | solution.py:23
  130.6 3.9 %collective-permute-start.15 = (bf16[4,128,128]{2,1,0:T(8,128)(2,1)S(1)}, bf16[4,128,128]{2,1,0:T(8,128)(2,1)S(1)}, u32[]{:S(2)}, u32[]{:S(2)}) collective-permute-start(bf16[4,128,128]{2,1,0:T(8,128)(2,1)S(1)} %fusion.4), channel_id=1, source_target_pairs={{0,4},{1,5},{2,6},{3,7},{4,0},{5,1},{6,2},{7,3},{8,12},{9,13},{10,... | collective-permute-start | bytes 393224 | tf_op jit(solution)/shard_map/ppermute | solution.py:23
  134.5 1.9 collective-permute-start.16
  136.5 1.0 collective-permute-done.15
  138.2 10.6 %all-to-all-start.2 = ((bf16[4,128,128]{2,1,0:T(8,128)(2,1)}), bf16[4,128,128]{2,1,0:T(8,128)(2,1)S(1)}, u32[]{:S(2)}, u32[]{:S(2)}) async-start(bf16[4,128,128]{2,1,0:T(8,128)(2,1)} %fusion.3), calls=%async_computation.2 | async-start | bytes 262144 | tf_op jit(solution)/shard_map/all_to_all | solution.py:27
  148.7 1.1 add_convert_fusion
  149.9 7.1 %all-to-all-done.2 = bf16[4,128,128]{2,1,0:T(8,128)(2,1)S(1)} async-done(((bf16[4,128,128]{2,1,0:T(8,128)(2,1)}), bf16[4,128,128]{2,1,0:T(8,128)(2,1)S(1)}, u32[]{:S(2)}, u32[]{:S(2)}) %all-to-all-start.2) | async-done | bytes 131104 | tf_op jit(solution)/shard_map/all_to_all | solution.py:27
  156.9 4.8 %all-to-all-start.4 = ((bf16[4,128,768]{2,1,0:T(8,128)(2,1)}), bf16[4,128,768]{2,1,0:T(8,128)(2,1)S(1)}, u32[]{:S(2)}, u32[]{:S(2)}) async-start(bf16[4,128,768]{2,1,0:T(8,128)(2,1)} %add_convert_fusion), calls=%async_computation.4 | async-start | bytes 1572864 | tf_op jit(solution)/shard_map/all_to_all | solution.py:27
  161.7 1.1 add_convert_fusion.1
  162.8 8.5 %all-to-all-done.4 = bf16[4,128,768]{2,1,0:T(8,128)(2,1)S(1)} async-done(((bf16[4,128,768]{2,1,0:T(8,128)(2,1)}), bf16[4,128,768]{2,1,0:T(8,128)(2,1)S(1)}, u32[]{:S(2)}, u32[]{:S(2)}) %all-to-all-start.4) | async-done | bytes 786464 | tf_op jit(solution)/shard_map/all_to_all | solution.py:27
  171.3 4.9 %all-to-all-start.3 = ((bf16[4,128,768]{2,1,0:T(8,128)(2,1)}), bf16[4,128,768]{2,1,0:T(8,128)(2,1)S(1)}, u32[]{:S(2)}, u32[]{:S(2)}) async-start(bf16[4,128,768]{2,1,0:T(8,128)(2,1)} %add_convert_fusion.1), calls=%async_computation.3 | async-start | bytes 1572864 | tf_op jit(solution)/shard_map/all_to_all | solution.py:27
  176.5 8.9 %collective-permute-start.18 = (bf16[128,768]{1,0:T(8,128)(2,1)S(1)}, bf16[128,768]{1,0:T(8,128)(2,1)S(1)}, u32[]{:S(2)}, u32[]{:S(2)}) collective-permute-start(bf16[128,768]{1,0:T(8,128)(2,1)S(1)} %reduce_sum.42), channel_id=1, source_target_pairs={{0,64},{32,96},{64,0},{96,32},{128,192},{160,224},{192,128},{224,1... | collective-permute-start | bytes 589832 | tf_op jit(solution)/shard_map/ppermute | solution.py:23
  186.2 17.2 %collective-permute-done.18 = bf16[128,768]{1,0:T(8,128)(2,1)S(1)} collective-permute-done((bf16[128,768]{1,0:T(8,128)(2,1)S(1)}, bf16[128,768]{1,0:T(8,128)(2,1)S(1)}, u32[]{:S(2)}, u32[]{:S(2)}) %collective-permute-start.18) | collective-permute-done | bytes 196640 | tf_op jit(solution)/shard_map/ppermute | solution.py:23
  203.4 0.7 fusion.7
  204.2 0.8 copy.22
  (50 shorter events, 3.9 us)
Async XLA Ops:
  0.6 0.8 copy-start.4
  1.5 0.8 copy-start.5
  2.3 0.8 copy-start.6
  3.2 20.0 %copy-start.7 = (bf16[1,256,64]{1,2,0:T(8,128)(2,1)S(1)}, bf16[1,256,64]{1,2,0:T(8,128)(2,1)}, u32[]{:S(2)}) copy-start(bf16[1,256,64]{1,2,0:T(8,128)(2,1)} %param.7) | copy-start | bytes 98308
  4.2 19.1 %copy-start.8 = (bf16[1,256,64]{1,2,0:T(8,128)(2,1)S(1)}, bf16[1,256,64]{1,2,0:T(8,128)(2,1)}, u32[]{:S(2)}) copy-start(bf16[1,256,64]{1,2,0:T(8,128)(2,1)} %param.8) | copy-start | bytes 98308
  4.2 31.1 %all-to-all-start = ((bf16[4,128,768]{2,1,0:T(8,128)(2,1)}), bf16[4,128,768]{2,1,0:T(8,128)(2,1)S(1)}, u32[]{:S(2)}, u32[]{:S(2)}) async-start(bf16[4,128,768]{2,1,0:T(8,128)(2,1)} %broadcast_in_dim.24), calls=%async_computation | async-start | bytes 1572864 | tf_op jit(solution)/shard_map/all_to_all | solution.py:27
  9.2 26.0 %collective-permute-start.9 = (bf16[128,768]{1,0:T(8,128)(2,1)S(1)}, bf16[128,768]{1,0:T(8,128)(2,1)S(1)}, u32[]{:S(2)}, u32[]{:S(2)}) collective-permute-start(bf16[128,768]{1,0:T(8,128)(2,1)S(1)} %shard_map.102), channel_id=1, source_target_pairs={{0,64},{32,96},{64,0},{96,32},{128,192},{160,224},{192,128},{224,1... | collective-permute-start | bytes 589832 | tf_op jit(solution)/shard_map/ppermute | solution.py:23
  36.2 21.9 %copy-start.9 = (s32[32]{0:T(128)S(1)}, s32[32]{0:T(128)}, u32[]{:S(2)}) copy-start(s32[32]{0:T(128)} %param.13) | copy-start | bytes 388
  36.2 31.6 %all-to-all-start.1 = ((bf16[4,128,768]{2,1,0:T(8,128)(2,1)}), bf16[4,128,768]{2,1,0:T(8,128)(2,1)S(1)}, u32[]{:S(2)}, u32[]{:S(2)}) async-start(bf16[4,128,768]{2,1,0:T(8,128)(2,1)} %broadcast_in_dim.25), calls=%async_computation.1 | async-start | bytes 1572864 | tf_op jit(solution)/shard_map/all_to_all | solution.py:27
  41.3 14.9 %collective-permute-start = (bf16[1,256,128]{2,1,0:T(8,128)(2,1)S(1)}, bf16[1,256,128]{2,1,0:T(8,128)(2,1)S(1)}, u32[]{:S(2)}, u32[]{:S(2)}) collective-permute-start(bf16[1,256,128]{2,1,0:T(8,128)(2,1)S(1)} %maximum_bitcast_fusion.2), channel_id=1, source_target_pairs={{0,16},{1,17},{2,18},{3,19},{4,20},{5,21},{6,22},{7,23},{8,24},{9,... | collective-permute-start | bytes 196616 | tf_op jit(solution)/shard_map/ppermute | solution.py:23
  56.2 7.8 %collective-permute-start.1 = (bf16[2,256,128]{2,1,0:T(8,128)(2,1)S(1)}, bf16[2,256,128]{2,1,0:T(8,128)(2,1)S(1)}, u32[]{:S(2)}, u32[]{:S(2)}) collective-permute-start(bf16[2,256,128]{2,1,0:T(8,128)(2,1)S(1)} %pad_maximum_fusion.1), channel_id=1, source_target_pairs={{0,8},{1,9},{2,10},{3,11},{4,12},{5,13},{6,14},{7,15},{8,0},{9,1},... | collective-permute-start | bytes 393224 | tf_op jit(solution)/shard_map/ppermute | solution.py:23
  64.0 13.7 %collective-permute-start.5 = (bf16[4,256,128]{2,1,0:T(8,128)(2,1)S(1)}, bf16[4,256,128]{2,1,0:T(8,128)(2,1)S(1)}, u32[]{:S(2)}, u32[]{:S(2)}) collective-permute-start(bf16[4,256,128]{2,1,0:T(8,128)(2,1)S(1)} %pad_maximum_fusion.lo0), channel_id=1, source_target_pairs={{0,4},{1,5},{2,6},{3,7},{4,0},{5,1},{6,2},{7,3},{8,12},{9,13},{10,... | collective-permute-start | bytes 786440 | tf_op jit(solution)/shard_map/ppermute | solution.py:23
  65.9 39.7 %collective-permute-start.10 = (bf16[4,128,768]{2,1,0:T(8,128)(2,1)S(1)}, bf16[4,128,768]{2,1,0:T(8,128)(2,1)S(1)}, u32[]{:S(2)}, u32[]{:S(2)}) collective-permute-start(bf16[4,128,768]{2,1,0:T(8,128)(2,1)S(1)} %all-to-all-done.w0), channel_id=1, source_target_pairs={{0,32},{32,0},{64,96},{96,64},{128,160},{160,128},{192,224},{224,1... | collective-permute-start | bytes 2359304 | tf_op jit(solution)/shard_map/ppermute | solution.py:23
  67.8 37.8 %collective-permute-start.11 = (bf16[4,128,768]{2,1,0:T(8,128)(2,1)S(1)}, bf16[4,128,768]{2,1,0:T(8,128)(2,1)S(1)}, u32[]{:S(2)}, u32[]{:S(2)}) collective-permute-start(bf16[4,128,768]{2,1,0:T(8,128)(2,1)S(1)} %all-to-all-done.1.w1), channel_id=1, source_target_pairs={{0,32},{32,0},{64,96},{96,64},{128,160},{160,128},{192,224},{224,1... | collective-permute-start | bytes 2359304 | tf_op jit(solution)/shard_map/ppermute | solution.py:23
  70.2 16.6 %collective-permute-start.4 = (bf16[4,256,128]{2,1,0:T(8,128)(2,1)S(1)}, bf16[4,256,128]{2,1,0:T(8,128)(2,1)S(1)}, u32[]{:S(2)}, u32[]{:S(2)}) collective-permute-start(bf16[4,256,128]{2,1,0:T(8,128)(2,1)S(1)} %pad_maximum_fusion.lo0), channel_id=1, source_target_pairs={{0,3},{1,2},{2,1},{3,0},{4,7},{5,6},{6,5},{7,4},{8,11},{9,10},{10,... | collective-permute-start | bytes 786440 | tf_op jit(solution)/shard_map/ppermute | solution.py:23
  74.9 16.9 %collective-permute-start.3 = (bf16[4,256,128]{2,1,0:T(8,128)(2,1)S(1)}, bf16[4,256,128]{2,1,0:T(8,128)(2,1)S(1)}, u32[]{:S(2)}, u32[]{:S(2)}) collective-permute-start(bf16[4,256,128]{2,1,0:T(8,128)(2,1)S(1)} %pad_maximum_fusion.lo0), channel_id=1, source_target_pairs={{0,2},{1,3},{2,0},{3,1},{4,6},{5,7},{6,4},{7,5},{8,10},{9,11},{10,... | collective-permute-start | bytes 786440 | tf_op jit(solution)/shard_map/ppermute | solution.py:23
  77.6 16.1 %collective-permute-start.2 = (bf16[4,256,128]{2,1,0:T(8,128)(2,1)S(1)}, bf16[4,256,128]{2,1,0:T(8,128)(2,1)S(1)}, u32[]{:S(2)}, u32[]{:S(2)}) collective-permute-start(bf16[4,256,128]{2,1,0:T(8,128)(2,1)S(1)} %pad_maximum_fusion.lo0), channel_id=1, source_target_pairs={{0,1},{1,0},{2,3},{3,2},{4,5},{5,4},{6,7},{7,6},{8,9},{9,8},{10,11... | collective-permute-start | bytes 786440 | tf_op jit(solution)/shard_map/ppermute | solution.py:23
  86.9 15.5 %collective-permute-start.8 = (bf16[4,256,128]{2,1,0:T(8,128)(2,1)S(1)}, bf16[4,256,128]{2,1,0:T(8,128)(2,1)S(1)}, u32[]{:S(2)}, u32[]{:S(2)}) collective-permute-start(bf16[4,256,128]{2,1,0:T(8,128)(2,1)S(1)} %collective-permute-done.5.hi0), channel_id=1, source_target_pairs={{0,3},{1,2},{2,1},{3,0},{4,7},{5,6},{6,5},{7,4},{8,11},{9,10},{10,... | collective-permute-start | bytes 786440 | tf_op jit(solution)/shard_map/ppermute | solution.py:23
  91.9 12.6 %collective-permute-start.7 = (bf16[4,256,128]{2,1,0:T(8,128)(2,1)S(1)}, bf16[4,256,128]{2,1,0:T(8,128)(2,1)S(1)}, u32[]{:S(2)}, u32[]{:S(2)}) collective-permute-start(bf16[4,256,128]{2,1,0:T(8,128)(2,1)S(1)} %collective-permute-done.5.hi0), channel_id=1, source_target_pairs={{0,2},{1,3},{2,0},{3,1},{4,6},{5,7},{6,4},{7,5},{8,10},{9,11},{10,... | collective-permute-start | bytes 786440 | tf_op jit(solution)/shard_map/ppermute | solution.py:23
  93.8 11.8 %collective-permute-start.6 = (bf16[4,256,128]{2,1,0:T(8,128)(2,1)S(1)}, bf16[4,256,128]{2,1,0:T(8,128)(2,1)S(1)}, u32[]{:S(2)}, u32[]{:S(2)}) collective-permute-start(bf16[4,256,128]{2,1,0:T(8,128)(2,1)S(1)} %collective-permute-done.5.hi0), channel_id=1, source_target_pairs={{0,1},{1,0},{2,3},{3,2},{4,5},{5,4},{6,7},{7,6},{8,9},{9,8},{10,11... | collective-permute-start | bytes 786440 | tf_op jit(solution)/shard_map/ppermute | solution.py:23
  96.7 0.7 copy-start.2
  105.6 1.0 copy-start.3
  110.8 1.4 copy-start
  112.3 12.2 %collective-permute-start.12 = (bf16[2,4,128,128]{3,2,1,0:T(8,128)(2,1)S(1)}, bf16[2,4,128,128]{3,2,1,0:T(8,128)(2,1)S(1)}, u32[]{:S(2)}, u32[]{:S(2)}) collective-permute-start(bf16[2,4,128,128]{3,2,1,0:T(8,128)(2,1)S(1)} %get-tuple-element.28), channel_id=1, source_target_pairs={{0,1},{1,0},{2,3},{3,2},{4,5},{5,4},{6,7},{7,6},{8,9},{9,8},{10,11... | collective-permute-start | bytes 786440 | tf_op jit(solution)/shard_map/ppermute | solution.py:23
  115.3 15.1 %collective-permute-start.14 = (bf16[2,4,128,128]{3,2,1,0:T(8,128)(2,1)S(1)}, bf16[2,4,128,128]{3,2,1,0:T(8,128)(2,1)S(1)}, u32[]{:S(2)}, u32[]{:S(2)}) collective-permute-start(bf16[2,4,128,128]{3,2,1,0:T(8,128)(2,1)S(1)} %get-tuple-element.29), channel_id=1, source_target_pairs={{0,3},{1,2},{2,1},{3,0},{4,7},{5,6},{6,5},{7,4},{8,11},{9,10},{10,... | collective-permute-start | bytes 786440 | tf_op jit(solution)/shard_map/ppermute | solution.py:23
  119.0 11.4 %collective-permute-start.13 = (bf16[2,4,128,128]{3,2,1,0:T(8,128)(2,1)S(1)}, bf16[2,4,128,128]{3,2,1,0:T(8,128)(2,1)S(1)}, u32[]{:S(2)}, u32[]{:S(2)}) collective-permute-start(bf16[2,4,128,128]{3,2,1,0:T(8,128)(2,1)S(1)} %get-tuple-element.30), channel_id=1, source_target_pairs={{0,2},{1,3},{2,0},{3,1},{4,6},{5,7},{6,4},{7,5},{8,10},{9,11},{10,... | collective-permute-start | bytes 786440 | tf_op jit(solution)/shard_map/ppermute | solution.py:23
  122.4 26.3 %copy-start.1 = (bf16[4,128,768]{2,1,0:T(8,128)(2,1)S(1)}, bf16[4,128,768]{2,1,0:T(8,128)(2,1)}, u32[]{:S(2)}) copy-start(bf16[4,128,768]{2,1,0:T(8,128)(2,1)} %copy-done) | copy-start | bytes 2359300
  122.4 26.3 %collective-permute-start.17 = (bf16[4,128,768]{2,1,0:T(8,128)(2,1)}, bf16[4,128,768]{2,1,0:T(8,128)(2,1)S(1)}, u32[]{:S(2)}, u32[]{:S(2)}) collective-permute-start(bf16[4,128,768]{2,1,0:T(8,128)(2,1)} %get-tuple-element.19), channel_id=1, source_target_pairs={{0,32},{32,0},{64,96},{96,64},{128,160},{160,128},{192,224},{224,1... | collective-permute-start | bytes 2359304 | tf_op jit(solution)/shard_map/ppermute | solution.py:23
  130.6 6.9 %collective-permute-start.15 = (bf16[4,128,128]{2,1,0:T(8,128)(2,1)S(1)}, bf16[4,128,128]{2,1,0:T(8,128)(2,1)S(1)}, u32[]{:S(2)}, u32[]{:S(2)}) collective-permute-start(bf16[4,128,128]{2,1,0:T(8,128)(2,1)S(1)} %fusion.4), channel_id=1, source_target_pairs={{0,4},{1,5},{2,6},{3,7},{4,0},{5,1},{6,2},{7,3},{8,12},{9,13},{10,... | collective-permute-start | bytes 393224 | tf_op jit(solution)/shard_map/ppermute | solution.py:23
  134.5 27.2 %collective-permute-start.16 = (bf16[4,128,768]{2,1,0:T(8,128)(2,1)}, bf16[4,128,768]{2,1,0:T(8,128)(2,1)S(1)}, u32[]{:S(2)}, u32[]{:S(2)}) collective-permute-start(bf16[4,128,768]{2,1,0:T(8,128)(2,1)} %get-tuple-element.17), channel_id=1, source_target_pairs={{0,32},{32,0},{64,96},{96,64},{128,160},{160,128},{192,224},{224,1... | collective-permute-start | bytes 2359304 | tf_op jit(solution)/shard_map/ppermute | solution.py:23
  138.2 18.8 %all-to-all-start.2 = ((bf16[4,128,128]{2,1,0:T(8,128)(2,1)}), bf16[4,128,128]{2,1,0:T(8,128)(2,1)S(1)}, u32[]{:S(2)}, u32[]{:S(2)}) async-start(bf16[4,128,128]{2,1,0:T(8,128)(2,1)} %fusion.3), calls=%async_computation.2 | async-start | bytes 262144 | tf_op jit(solution)/shard_map/all_to_all | solution.py:27
  156.9 14.4 %all-to-all-start.4 = ((bf16[4,128,768]{2,1,0:T(8,128)(2,1)}), bf16[4,128,768]{2,1,0:T(8,128)(2,1)S(1)}, u32[]{:S(2)}, u32[]{:S(2)}) async-start(bf16[4,128,768]{2,1,0:T(8,128)(2,1)} %add_convert_fusion), calls=%async_computation.4 | async-start | bytes 1572864 | tf_op jit(solution)/shard_map/all_to_all | solution.py:27
  171.3 14.8 %all-to-all-start.3 = ((bf16[4,128,768]{2,1,0:T(8,128)(2,1)}), bf16[4,128,768]{2,1,0:T(8,128)(2,1)S(1)}, u32[]{:S(2)}, u32[]{:S(2)}) async-start(bf16[4,128,768]{2,1,0:T(8,128)(2,1)} %add_convert_fusion.1), calls=%async_computation.3 | async-start | bytes 1572864 | tf_op jit(solution)/shard_map/all_to_all | solution.py:27
  176.5 26.9 %collective-permute-start.18 = (bf16[128,768]{1,0:T(8,128)(2,1)S(1)}, bf16[128,768]{1,0:T(8,128)(2,1)S(1)}, u32[]{:S(2)}, u32[]{:S(2)}) collective-permute-start(bf16[128,768]{1,0:T(8,128)(2,1)S(1)} %reduce_sum.42), channel_id=1, source_target_pairs={{0,64},{32,96},{64,0},{96,32},{128,192},{160,224},{192,128},{224,1... | collective-permute-start | bytes 589832 | tf_op jit(solution)/shard_map/ppermute | solution.py:23
where the time goes:
time: 206 us; the launch traced here: 205 us
  starting transfers between devices  111 us (54%)
  waiting for transfers between devices  73.5 us (36%)
  local copies, waits for them, and re-layouts  8.59 us (4%)
  Pallas kernels  5.64 us (3%)
  other arithmetic  4.27 us (2%)
  between operations  2.34 us (1%)
    ppermute x19, starting transfers between devices, swap(): lax.ppermute(v, axis, [(k, k ^ offset) for k in range(lax.axis_size(axis))])  80.3 us
    ppermute x19, waiting for transfers between devices, swap(): lax.ppermute(v, axis, [(k, k ^ offset) for k in range(lax.axis_size(axis))])  58 us
    all_to_all x5, starting transfers between devices, exchange(): return lax.all_to_all(v, axis, 0, 0, axis_index_groups=groups, tiled=True)  30.3 us
    all_to_all x5, waiting for transfers between devices, exchange(): return lax.all_to_all(v, axis, 0, 0, axis_index_groups=groups, tiled=True)  15.6 us
    unnamed x24, local copies, waits for them, and re-layouts  5.86 us
    pallas_call x1, Pallas kernels, step(): call(forward_kernel, [grad] * 4 + [sds(TOK, 2 * BLK)], 2, 12, [pltpu.VMEM...  4.21 us
  transfers between devices with their start and end apart: 24, of which 12 were waited for; matrix products, arithmetic and copies ran while one was open for 3% of the time, Pallas kernels for 0%

commit v1 on v0

--- a/solution.py
+++ b/solution.py
@@ -10,7 +10,7 @@
 LANES = 128
 BLK = 256
 Y_GROUPS = [[4 * y + r for y in range(4)] for r in range(4)]
-Z_GROUPS = [[8 * q + r for q in range(4)] for r in range(8)]
+Z_OFFSETS = (0, 4, 2, 6, 1, 5, 3, 7)
 
 
 VMEM = pl.BlockSpec(memory_space=pltpu.VMEM)
@@ -39,15 +39,14 @@
     return (lax.broadcasted_iota(jnp.int32, shape, 1) < LANES // 2) == (parity == 0)
 
 
-def forward_kernel(place, keep_ref, lo0, lo1, lo2, lo3, hi0, hi1, hi2, hi3, w0, w1, w2, w3,
+def forward_kernel(place, keep_ref, x0, x1, x2, x3, w0, w1, w2, w3,
                    own0, own1, away0, away1, dgu, tok, cot, hid):
     side, core, parity, quarter = place[0], place[1], place[2], place[3]
     mask = halves_mask((TOK, LANES), parity)
-    pairs = ((lo0, lo1, 0, 0), (lo2, lo3, 1, 0), (hi0, hi1, 0, 1), (hi2, hi3, 1, 1))
-    for even, odd, half, turn in pairs:
-        chunk = (half ^ core) * 2 + (turn ^ side)
-        for s, q in enumerate((0, 2, 1, 3)):
-            lanes = pl.ds(pl.multiple_of((chunk * 4 + (quarter ^ q)) * LANES, LANES), LANES)
+    for half, (even, odd) in enumerate(((x0, x1), (x2, x3))):
+        for s, a in enumerate(Z_OFFSETS):
+            chunk = (half ^ core) * 2 + (a % 2 ^ side)
+            lanes = pl.ds(pl.multiple_of((chunk * 4 + (quarter ^ a // 2)) * LANES, LANES), LANES)
             e, f = even[s], odd[s]
             tok[:, lanes] = jnp.where(mask, e, f)
             cot[:, lanes] = jnp.where(mask, f, e)
@@ -83,20 +82,30 @@
     out[64:, 2 * BLK :] = turned[:64]
 
 
-def token_grads_kernel(place, dgu, w0, w1, w2, w3, out):
-    side, core, parity = place[0], place[1], place[2]
+def token_grads_kernel(place, dgu, w0, w1, w2, w3, r0, r1, r2, r3):
+    side, core, parity, quarter = place[0], place[1], place[2], place[3]
     mask = halves_mask((TOK // 2, LANES), parity)
     dims = (((1,), (1,)), ((), ()))
-    for k, w in enumerate((w0, w1, w2, w3)):
-        wk = w[...].reshape(512, 3 * BLK)[:, : 2 * BLK]
-        part = lax.dot_general(dgu[...], wk, dims, preferred_element_type=F32)
-        x, turn = 2 * (k // 2 ^ core), k % 2 ^ side
-        for q in range(4):
-            block = part[:, q * LANES : (q + 1) * LANES]
-            top = block[: TOK // 2]
-            low = pltpu.roll(block[TOK // 2 :], LANES // 2, 1)
-            out[x, turn, q] = jnp.where(mask, top, low).astype(BF16)
-            out[x + 1, turn, q] = jnp.where(mask, low, top).astype(BF16)
+
+    def half(weights, same, other):
+        for k, w in enumerate(weights):
+            wk = w[...].reshape(512, 3 * BLK)[:, : 2 * BLK]
+            part = lax.dot_general(dgu[...], wk, dims, preferred_element_type=F32)
+            for y in range(4):
+                q = quarter ^ y
+                at = (k ^ side) * 4 + (q & 1) * 2 + lax.shift_right_logical(q, 1)
+                block = part[:, y * LANES : (y + 1) * LANES]
+                top = block[: TOK // 2]
+                low = pltpu.roll(block[TOK // 2 :], LANES // 2, 1)
+                same[at] = jnp.where(mask, top, low).astype(BF16)
+                other[at] = jnp.where(mask, low, top).astype(BF16)
+
+    for turn, (first, second) in enumerate((((w0, w1), (w2, w3)), ((w2, w3), (w0, w1)))):
+
+        @pl.when(core == turn)
+        def _(first=first, second=second):
+            half(first, r0, r1)
+            half(second, r2, r3)
 
 
 def call(kernel, outs, n_smem, n_in, scratch, mib):
@@ -135,32 +144,33 @@
     w_own = gather(shard, "cand", Y_GROUPS)
     pieces = jnp.concatenate([pieces, swap(pieces, "hid", 8)], axis=0)
     pieces, place, keep = lax.optimization_barrier((pieces, place, keep))
-    others = swap(pieces, "hid", 4)
-    los = [pieces] + [swap(pieces, "hid", b) for b in (1, 2, 3)]
-    his = [others] + [swap(others, "hid", b) for b in (1, 2, 3)]
+    pieces = jnp.concatenate([pieces, swap(pieces, "hid", 4)], axis=0)
+    xs = [pieces] + [swap(pieces, "hid", b) for b in (1, 2, 3)]
     w_far = gather(far, "cand", Y_GROUPS)
     weights = [w_own, w_far, swap(w_own, "cand", 1), swap(w_far, "cand", 1)]
 
     grad = sds(4, 128, 3 * BLK)
     own0, own1, away0, away1, dgu = call(
-        forward_kernel, [grad] * 4 + [sds(TOK, 2 * BLK)], 2, 12,
+        forward_kernel, [grad] * 4 + [sds(TOK, 2 * BLK)], 2, 8,
         [pltpu.VMEM((TOK, 2048), BF16)] * 2 + [pltpu.VMEM((TOK, BLK), BF16)], 12,
-    )(place, keep, *los, *his, *weights)
-    (parts,) = call(token_grads_kernel, [sds(4, 2, 4, 128, 128)], 1, 5, [], 8)(place, dgu, *weights)
+    )(place, keep, *xs, *weights)
+    r0, *rs = call(token_grads_kernel, [sds(8, 128, 128)] * 4, 1, 5, [], 8)(place, dgu, *weights)
 
     both1 = own1.astype(F32) + swap(away1, "cand", 1).astype(F32)
     total1 = total(exchange(both1.astype(BF16), "cand", Y_GROUPS))
     arrived0 = swap(away0, "cand", 1)
     both0 = (own0.astype(F32) + arrived0.astype(F32)).astype(BF16)
     grads = total(exchange(both0, "cand", Y_GROUPS))
-    grads = grads + swap(total1.astype(BF16), "cand", 2).astype(F32)
+    last = swap(total1.astype(BF16), "cand", 2)
+    grads = lax.optimization_barrier(grads) + last.astype(F32)
 
-    arrived = [swap(parts[b], "hid", b) for b in (1, 2, 3)]
-    part = parts[0].astype(F32)
-    for r in arrived:
-        part = part + r.astype(F32)
-    part = part[0] + swap(part[1].astype(BF16), "hid", 4).astype(F32)
-    part = total(exchange(part.astype(BF16), "hid", Z_GROUPS))
+    part = r0.astype(F32)
+    for b, r in zip((1, 2, 3), rs):
+        part = part + swap(r, "hid", b).astype(F32)
+    for dist in (1, 2, 4):
+        n = part.shape[0] // 2
+        part = part[:n] + swap(part[n:].astype(BF16), "hid", 4 * dist).astype(F32)
+    part = part[0]
     left, right = part[:, :64], part[:, 64:]
     top, low = jnp.where(parity == 0, left, right), jnp.where(parity == 0, right, left)
     grad_tokens = jnp.concatenate([top, low], axis=0)[None]

time: 206 us -> 185 us (0.90)
  the two profiles are of different devices: /device:TPU:72 before, /device:TPU:104 now
where the time goes in v1:
time: 185 us; the launch traced here: 184 us
  starting transfers between devices  97.8 us (53%)
  waiting for transfers between devices  68 us (37%)
  local copies, waits for them, and re-layouts  6.92 us (4%)
  Pallas kernels  5.69 us (3%)
  other arithmetic  3.61 us (2%)
  between operations  2.31 us (1%)
    ppermute x18, starting transfers between devices, swap(): lax.ppermute(v, axis, [(k, k ^ offset) for k in range(lax.axis_size(axis))])  78.3 us
    ppermute x18, waiting for transfers between devices, swap(): lax.ppermute(v, axis, [(k, k ^ offset) for k in range(lax.axis_size(axis))])  67.9 us
    all_to_all x4, starting transfers between devices, exchange(): return lax.all_to_all(v, axis, 0, 0, axis_index_groups=groups, tiled=True)  19.6 us
    unnamed x17, local copies, waits for them, and re-layouts  4.24 us
    pallas_call x1, Pallas kernels, step(): call(forward_kernel, [grad] * 4 + [sds(TOK, 2 * BLK)], 2, 8, [pltpu.VMEM(...  4.21 us
  transfers between devices with their start and end apart: 22, of which 10 were waited for; matrix products, arithmetic and copies ran while one was open for 3% of the time, Pallas kernels for 1%

profile of v1, /device:TPU:104, one launch (start us, length us, event | category | flops | bytes accessed | tf_op | source)
XLA Modules:
  0.0 184.3 jit_solution(517031885846464388)
XLA Ops:
  0.6 0.8 copy-done
  1.5 0.8 copy-done.1
  2.3 0.8 copy-done.2
  3.2 0.9 broadcast_in_dim.24
  4.2 5.0 %all-to-all-start = ((bf16[4,128,768]{2,1,0:T(8,128)(2,1)}), bf16[4,128,768]{2,1,0:T(8,128)(2,1)S(1)}, u32[]{:S(2)}, u32[]{:S(2)}) async-start(bf16[4,128,768]{2,1,0:T(8,128)(2,1)} %broadcast_in_dim.24), calls=%async_computation | async-start | bytes 1572864 | tf_op jit(solution)/shard_map/all_to_all | solution.py:27
  9.2 13.0 %collective-permute-start.6 = (bf16[128,768]{1,0:T(8,128)(2,1)S(1)}, bf16[128,768]{1,0:T(8,128)(2,1)S(1)}, u32[]{:S(2)}, u32[]{:S(2)}) collective-permute-start(bf16[128,768]{1,0:T(8,128)(2,1)S(1)} %shard_map.102), channel_id=1, source_target_pairs={{0,64},{32,96},{64,0},{96,32},{128,192},{160,224},{192,128},{224,1... | collective-permute-start | bytes 589832 | tf_op jit(solution)/shard_map/ppermute | solution.py:23
  22.4 0.1 copy.19
  22.6 4.3 %collective-permute-start = (bf16[1,256,128]{2,1,0:T(8,128)(2,1)S(1)}, bf16[1,256,128]{2,1,0:T(8,128)(2,1)S(1)}, u32[]{:S(2)}, u32[]{:S(2)}) collective-permute-start(bf16[1,256,128]{2,1,0:T(8,128)(2,1)S(1)} %maximum_bitcast_fusion.2), channel_id=1, source_target_pairs={{0,16},{1,17},{2,18},{3,19},{4,20},{5,21},{6,22},{7,23},{8,24},{9,... | collective-permute-start | bytes 196616 | tf_op jit(solution)/shard_map/ppermute | solution.py:23
  26.9 6.9 %collective-permute-done.6 = bf16[128,768]{1,0:T(8,128)(2,1)S(1)} collective-permute-done((bf16[128,768]{1,0:T(8,128)(2,1)S(1)}, bf16[128,768]{1,0:T(8,128)(2,1)S(1)}, u32[]{:S(2)}, u32[]{:S(2)}) %collective-permute-start.6) | collective-permute-done | bytes 196640 | tf_op jit(solution)/shard_map/ppermute | solution.py:23
  33.9 0.9 broadcast_in_dim.25
  34.8 4.9 %all-to-all-start.1 = ((bf16[4,128,768]{2,1,0:T(8,128)(2,1)}), bf16[4,128,768]{2,1,0:T(8,128)(2,1)S(1)}, u32[]{:S(2)}, u32[]{:S(2)}) async-start(bf16[4,128,768]{2,1,0:T(8,128)(2,1)} %broadcast_in_dim.25), calls=%async_computation.1 | async-start | bytes 1572864 | tf_op jit(solution)/shard_map/all_to_all | solution.py:27
  39.7 4.1 %collective-permute-done = bf16[1,256,128]{2,1,0:T(8,128)(2,1)S(1)} collective-permute-done((bf16[1,256,128]{2,1,0:T(8,128)(2,1)S(1)}, bf16[1,256,128]{2,1,0:T(8,128)(2,1)S(1)}, u32[]{:S(2)}, u32[]{:S(2)}) %collective-permute-start) | collective-permute-done | bytes 65568 | tf_op jit(solution)/shard_map/ppermute | solution.py:23
  43.8 3.2 %collective-permute-start.1 = (bf16[2,256,128]{2,1,0:T(8,128)(2,1)S(1)}, bf16[2,256,128]{2,1,0:T(8,128)(2,1)S(1)}, u32[]{:S(2)}, u32[]{:S(2)}) collective-permute-start(bf16[2,256,128]{2,1,0:T(8,128)(2,1)S(1)} %pad_maximum_fusion.1), channel_id=1, source_target_pairs={{0,8},{1,9},{2,10},{3,11},{4,12},{5,13},{6,14},{7,15},{8,0},{9,1},... | collective-permute-start | bytes 393224 | tf_op jit(solution)/shard_map/ppermute | solution.py:23
  47.0 0.6 fusion.1
  49.1 4.2 %collective-permute-done.1 = bf16[2,256,128]{2,1,0:T(8,128)(2,1)S(1)} collective-permute-done((bf16[2,256,128]{2,1,0:T(8,128)(2,1)S(1)}, bf16[2,256,128]{2,1,0:T(8,128)(2,1)S(1)}, u32[]{:S(2)}, u32[]{:S(2)}) %collective-permute-start.1) | collective-permute-done | bytes 131104 | tf_op jit(solution)/shard_map/ppermute | solution.py:23
  53.3 4.6 %collective-permute-start.2 = (bf16[4,256,128]{2,1,0:T(8,128)(2,1)S(1)}, bf16[4,256,128]{2,1,0:T(8,128)(2,1)S(1)}, u32[]{:S(2)}, u32[]{:S(2)}) collective-permute-start(bf16[4,256,128]{2,1,0:T(8,128)(2,1)S(1)} %pad_maximum_fusion), channel_id=1, source_target_pairs={{0,4},{1,5},{2,6},{3,7},{4,0},{5,1},{6,2},{7,3},{8,12},{9,13},{10,... | collective-permute-start | bytes 786440 | tf_op jit(solution)/shard_map/ppermute | solution.py:23
  57.9 1.9 %collective-permute-start.7 = (bf16[4,128,768]{2,1,0:T(8,128)(2,1)S(1)}, bf16[4,128,768]{2,1,0:T(8,128)(2,1)S(1)}, u32[]{:S(2)}, u32[]{:S(2)}) collective-permute-start(bf16[4,128,768]{2,1,0:T(8,128)(2,1)S(1)} %all-to-all-done.w0), channel_id=1, source_target_pairs={{0,32},{32,0},{64,96},{96,64},{128,160},{160,128},{192,224},{224,1... | collective-permute-start | bytes 2359304 | tf_op jit(solution)/shard_map/ppermute | solution.py:23
  59.8 2.4 %collective-permute-start.8 = (bf16[4,128,768]{2,1,0:T(8,128)(2,1)S(1)}, bf16[4,128,768]{2,1,0:T(8,128)(2,1)S(1)}, u32[]{:S(2)}, u32[]{:S(2)}) collective-permute-start(bf16[4,128,768]{2,1,0:T(8,128)(2,1)S(1)} %all-to-all-done.1.w1), channel_id=1, source_target_pairs={{0,32},{32,0},{64,96},{96,64},{128,160},{160,128},{192,224},{224,1... | collective-permute-start | bytes 2359304 | tf_op jit(solution)/shard_map/ppermute | solution.py:23
  62.3 0.3 collective-permute-done.2
  62.6 4.7 %collective-permute-start.5 = (bf16[8,256,128]{2,1,0:T(8,128)(2,1)S(1)}, bf16[8,256,128]{2,1,0:T(8,128)(2,1)S(1)}, u32[]{:S(2)}, u32[]{:S(2)}) collective-permute-start(bf16[8,256,128]{2,1,0:T(8,128)(2,1)S(1)} %constant_dynamic-update-slice_fusion.x0), channel_id=1, source_target_pairs={{0,3},{1,2},{2,1},{3,0},{4,7},{5,6},{6,5},{7,4},{8,11},{9,10},{10,... | collective-permute-start | bytes 1572872 | tf_op jit(solution)/shard_map/ppermute | solution.py:23
  67.3 2.7 %collective-permute-start.4 = (bf16[8,256,128]{2,1,0:T(8,128)(2,1)S(1)}, bf16[8,256,128]{2,1,0:T(8,128)(2,1)S(1)}, u32[]{:S(2)}, u32[]{:S(2)}) collective-permute-start(bf16[8,256,128]{2,1,0:T(8,128)(2,1)S(1)} %constant_dynamic-update-slice_fusion.x0), channel_id=1, source_target_pairs={{0,2},{1,3},{2,0},{3,1},{4,6},{5,7},{6,4},{7,5},{8,10},{9,11},{10,... | collective-permute-start | bytes 1572872 | tf_op jit(solution)/shard_map/ppermute | solution.py:23
  70.0 2.4 %collective-permute-start.3 = (bf16[8,256,128]{2,1,0:T(8,128)(2,1)S(1)}, bf16[8,256,128]{2,1,0:T(8,128)(2,1)S(1)}, u32[]{:S(2)}, u32[]{:S(2)}) collective-permute-start(bf16[8,256,128]{2,1,0:T(8,128)(2,1)S(1)} %constant_dynamic-update-slice_fusion.x0), channel_id=1, source_target_pairs={{0,1},{1,0},{2,3},{3,2},{4,5},{5,4},{6,7},{7,6},{8,9},{9,8},{10,11... | collective-permute-start | bytes 1572872 | tf_op jit(solution)/shard_map/ppermute | solution.py:23
  72.5 18.0 %collective-permute-done.5.x3 = bf16[8,256,128]{2,1,0:T(8,128)(2,1)S(1)} collective-permute-done((bf16[8,256,128]{2,1,0:T(8,128)(2,1)S(1)}, bf16[8,256,128]{2,1,0:T(8,128)(2,1)S(1)}, u32[]{:S(2)}, u32[]{:S(2)}) %collective-permute-start.5) | collective-permute-done | bytes 524320 | tf_op jit(solution)/shard_map/ppermute | solution.py:23
  90.5 2.5 %collective-permute-done.3.x1 = bf16[8,256,128]{2,1,0:T(8,128)(2,1)S(1)} collective-permute-done((bf16[8,256,128]{2,1,0:T(8,128)(2,1)S(1)}, bf16[8,256,128]{2,1,0:T(8,128)(2,1)S(1)}, u32[]{:S(2)}, u32[]{:S(2)}) %collective-permute-start.3) | collective-permute-done | bytes 524320 | tf_op jit(solution)/shard_map/ppermute | solution.py:23
  93.1 4.2 %shard_map.103 = (bf16[4,128,768]{2,1,0:T(8,128)(2,1)S(1)}, bf16[4,128,768]{2,1,0:T(8,128)(2,1)S(1)}, bf16[4,128,768]{2,1,0:T(8,128)(2,1)}, bf16[4,128,768]{2,1,0:T(8,128)(2,1)S(1)}, bf16[256,512]{1,0:T(8,128)(2,1)S(1)}) custom-call(s32[4]{0:T(128)S(1)} %pad_add_fusion.place, f32[1]{0:T(128)} %bitcast.8.keep_ref, ...), custom_call_target="tpu_custom_call" | custom-call | tf_op jit(solution)/shard_map/pallas_call | solution.py:153
  97.3 1.9 %collective-permute-start.16 = (bf16[4,128,768]{2,1,0:T(8,128)(2,1)S(1)}, bf16[4,128,768]{2,1,0:T(8,128)(2,1)S(1)}, u32[]{:S(2)}, u32[]{:S(2)}) collective-permute-start(bf16[4,128,768]{2,1,0:T(8,128)(2,1)S(1)} %get-tuple-element.27), channel_id=1, source_target_pairs={{0,32},{32,0},{64,96},{96,64},{128,160},{160,128},{192,224},{224,1... | collective-permute-start | bytes 2359304 | tf_op jit(solution)/shard_map/ppermute | solution.py:23
  99.2 1.4 shard_map.104
  100.6 3.4 %collective-permute-start.9 = (bf16[8,128,128]{2,1,0:T(8,128)(2,1)S(1)}, bf16[8,128,128]{2,1,0:T(8,128)(2,1)S(1)}, u32[]{:S(2)}, u32[]{:S(2)}) collective-permute-start(bf16[8,128,128]{2,1,0:T(8,128)(2,1)S(1)} %get-tuple-element.21), channel_id=1, source_target_pairs={{0,1},{1,0},{2,3},{3,2},{4,5},{5,4},{6,7},{7,6},{8,9},{9,8},{10,11... | collective-permute-start | bytes 786440 | tf_op jit(solution)/shard_map/ppermute | solution.py:23
  104.0 4.6 %collective-permute-start.10 = (bf16[8,128,128]{2,1,0:T(8,128)(2,1)S(1)}, bf16[8,128,128]{2,1,0:T(8,128)(2,1)S(1)}, u32[]{:S(2)}, u32[]{:S(2)}) collective-permute-start(bf16[8,128,128]{2,1,0:T(8,128)(2,1)S(1)} %get-tuple-element.22), channel_id=1, source_target_pairs={{0,2},{1,3},{2,0},{3,1},{4,6},{5,7},{6,4},{7,5},{8,10},{9,11},{10,... | collective-permute-start | bytes 786440 | tf_op jit(solution)/shard_map/ppermute | solution.py:23
  108.7 2.4 %collective-permute-start.11 = (bf16[8,128,128]{2,1,0:T(8,128)(2,1)S(1)}, bf16[8,128,128]{2,1,0:T(8,128)(2,1)S(1)}, u32[]{:S(2)}, u32[]{:S(2)}) collective-permute-start(bf16[8,128,128]{2,1,0:T(8,128)(2,1)S(1)} %get-tuple-element.23), channel_id=1, source_target_pairs={{0,3},{1,2},{2,1},{3,0},{4,7},{5,6},{6,5},{7,4},{8,11},{9,10},{10,... | collective-permute-start | bytes 786440 | tf_op jit(solution)/shard_map/ppermute | solution.py:23
  111.0 1.9 %collective-permute-start.15 = (bf16[4,128,768]{2,1,0:T(8,128)(2,1)}, bf16[4,128,768]{2,1,0:T(8,128)(2,1)S(1)}, u32[]{:S(2)}, u32[]{:S(2)}) collective-permute-start(bf16[4,128,768]{2,1,0:T(8,128)(2,1)} %get-tuple-element.25), channel_id=1, source_target_pairs={{0,32},{32,0},{64,96},{96,64},{128,160},{160,128},{192,224},{224,1... | collective-permute-start | bytes 2359304 | tf_op jit(solution)/shard_map/ppermute | solution.py:23
  113.0 6.1 %collective-permute-done.10 = bf16[8,128,128]{2,1,0:T(8,128)(2,1)S(1)} collective-permute-done((bf16[8,128,128]{2,1,0:T(8,128)(2,1)S(1)}, bf16[8,128,128]{2,1,0:T(8,128)(2,1)S(1)}, u32[]{:S(2)}, u32[]{:S(2)}) %collective-permute-start.10) | collective-permute-done | bytes 262176 | tf_op jit(solution)/shard_map/ppermute | solution.py:23
  119.1 5.5 %collective-permute-done.11 = bf16[8,128,128]{2,1,0:T(8,128)(2,1)S(1)} collective-permute-done((bf16[8,128,128]{2,1,0:T(8,128)(2,1)S(1)}, bf16[8,128,128]{2,1,0:T(8,128)(2,1)S(1)}, u32[]{:S(2)}, u32[]{:S(2)}) %collective-permute-start.11) | collective-permute-done | bytes 262176 | tf_op jit(solution)/shard_map/ppermute | solution.py:23
  124.6 0.1 convert_add_fusion
  124.8 1.9 %collective-permute-start.12 = (bf16[4,128,128]{2,1,0:T(8,128)(2,1)S(1)}, bf16[4,128,128]{2,1,0:T(8,128)(2,1)S(1)}, u32[]{:S(2)}, u32[]{:S(2)}) collective-permute-start(bf16[4,128,128]{2,1,0:T(8,128)(2,1)S(1)} %slice.78), channel_id=1, source_target_pairs={{0,4},{1,5},{2,6},{3,7},{4,0},{5,1},{6,2},{7,3},{8,12},{9,13},{10,... | collective-permute-start | bytes 393224 | tf_op jit(solution)/shard_map/ppermute | solution.py:23
  126.7 1.1 add_convert_fusion
  127.9 4.8 %all-to-all-start.3 = ((bf16[4,128,768]{2,1,0:T(8,128)(2,1)}), bf16[4,128,768]{2,1,0:T(8,128)(2,1)S(1)}, u32[]{:S(2)}, u32[]{:S(2)}) async-start(bf16[4,128,768]{2,1,0:T(8,128)(2,1)} %add_convert_fusion), calls=%async_computation.3 | async-start | bytes 1572864 | tf_op jit(solution)/shard_map/all_to_all | solution.py:27
  132.7 6.4 %collective-permute-start.13 = (bf16[2,128,128]{2,1,0:T(8,128)(2,1)S(1)}, bf16[2,128,128]{2,1,0:T(8,128)(2,1)S(1)}, u32[]{:S(2)}, u32[]{:S(2)}) collective-permute-start(bf16[2,128,128]{2,1,0:T(8,128)(2,1)S(1)} %slice.79), channel_id=1, source_target_pairs={{0,8},{1,9},{2,10},{3,11},{4,12},{5,13},{6,14},{7,15},{8,0},{9,1},... | collective-permute-start | bytes 196616 | tf_op jit(solution)/shard_map/ppermute | solution.py:23
  139.2 2.9 %collective-permute-done.13 = bf16[2,128,128]{2,1,0:T(8,128)(2,1)S(1)} collective-permute-done((bf16[2,128,128]{2,1,0:T(8,128)(2,1)S(1)}, bf16[2,128,128]{2,1,0:T(8,128)(2,1)S(1)}, u32[]{:S(2)}, u32[]{:S(2)}) %collective-permute-start.13) | collective-permute-done | bytes 65568 | tf_op jit(solution)/shard_map/ppermute | solution.py:23
  142.1 7.2 %collective-permute-start.14 = (bf16[1,128,128]{2,1,0:T(8,128)(2,1)S(1)}, bf16[1,128,128]{2,1,0:T(8,128)(2,1)S(1)}, u32[]{:S(2)}, u32[]{:S(2)}) collective-permute-start(bf16[1,128,128]{2,1,0:T(8,128)(2,1)S(1)} %slice.80), channel_id=1, source_target_pairs={{0,16},{1,17},{2,18},{3,19},{4,20},{5,21},{6,22},{7,23},{8,24},{9,... | collective-permute-start | bytes 98312 | tf_op jit(solution)/shard_map/ppermute | solution.py:23
  149.3 1.1 add_convert_fusion.1
  150.4 4.8 %all-to-all-start.2 = ((bf16[4,128,768]{2,1,0:T(8,128)(2,1)}), bf16[4,128,768]{2,1,0:T(8,128)(2,1)S(1)}, u32[]{:S(2)}, u32[]{:S(2)}) async-start(bf16[4,128,768]{2,1,0:T(8,128)(2,1)} %add_convert_fusion.1), calls=%async_computation.2 | async-start | bytes 1572864 | tf_op jit(solution)/shard_map/all_to_all | solution.py:27
  155.3 0.1 reduce_sum.32
  155.5 9.2 %collective-permute-start.17 = (bf16[128,768]{1,0:T(8,128)(2,1)S(1)}, bf16[128,768]{1,0:T(8,128)(2,1)S(1)}, u32[]{:S(2)}, u32[]{:S(2)}) collective-permute-start(bf16[128,768]{1,0:T(8,128)(2,1)S(1)} %reduce_sum.32), channel_id=1, source_target_pairs={{0,64},{32,96},{64,0},{96,32},{128,192},{160,224},{192,128},{224,1... | collective-permute-start | bytes 589832 | tf_op jit(solution)/shard_map/ppermute | solution.py:23
  164.7 0.7 copy.22
  165.5 17.2 %collective-permute-done.17 = bf16[128,768]{1,0:T(8,128)(2,1)S(1)} collective-permute-done((bf16[128,768]{1,0:T(8,128)(2,1)S(1)}, bf16[128,768]{1,0:T(8,128)(2,1)S(1)}, u32[]{:S(2)}, u32[]{:S(2)}) %collective-permute-start.17) | collective-permute-done | bytes 196640 | tf_op jit(solution)/shard_map/ppermute | solution.py:23
  182.8 0.7 fusion.3
  183.6 0.8 copy.23
  (42 shorter events, 0.9 us)
Async XLA Ops:
  0.6 0.8 copy-start
  1.5 0.8 copy-start.1
  2.3 0.8 copy-start.2
  4.2 18.1 %copy-start.3 = (bf16[1,256,64]{1,2,0:T(8,128)(2,1)S(1)}, bf16[1,256,64]{1,2,0:T(8,128)(2,1)}, u32[]{:S(2)}) copy-start(bf16[1,256,64]{1,2,0:T(8,128)(2,1)} %param.7) | copy-start | bytes 98308
  4.2 18.2 %copy-start.4 = (bf16[1,256,64]{1,2,0:T(8,128)(2,1)S(1)}, bf16[1,256,64]{1,2,0:T(8,128)(2,1)}, u32[]{:S(2)}) copy-start(bf16[1,256,64]{1,2,0:T(8,128)(2,1)} %param.8) | copy-start | bytes 98308
  4.2 29.7 %all-to-all-start = ((bf16[4,128,768]{2,1,0:T(8,128)(2,1)}), bf16[4,128,768]{2,1,0:T(8,128)(2,1)S(1)}, u32[]{:S(2)}, u32[]{:S(2)}) async-start(bf16[4,128,768]{2,1,0:T(8,128)(2,1)} %broadcast_in_dim.24), calls=%async_computation | async-start | bytes 1572864 | tf_op jit(solution)/shard_map/all_to_all | solution.py:27
  9.2 24.7 %collective-permute-start.6 = (bf16[128,768]{1,0:T(8,128)(2,1)S(1)}, bf16[128,768]{1,0:T(8,128)(2,1)S(1)}, u32[]{:S(2)}, u32[]{:S(2)}) collective-permute-start(bf16[128,768]{1,0:T(8,128)(2,1)S(1)} %shard_map.102), channel_id=1, source_target_pairs={{0,64},{32,96},{64,0},{96,32},{128,192},{160,224},{192,128},{224,1... | collective-permute-start | bytes 589832 | tf_op jit(solution)/shard_map/ppermute | solution.py:23
  22.6 21.2 %collective-permute-start = (bf16[1,256,128]{2,1,0:T(8,128)(2,1)S(1)}, bf16[1,256,128]{2,1,0:T(8,128)(2,1)S(1)}, u32[]{:S(2)}, u32[]{:S(2)}) collective-permute-start(bf16[1,256,128]{2,1,0:T(8,128)(2,1)S(1)} %maximum_bitcast_fusion.2), channel_id=1, source_target_pairs={{0,16},{1,17},{2,18},{3,19},{4,20},{5,21},{6,22},{7,23},{8,24},{9,... | collective-permute-start | bytes 196616 | tf_op jit(solution)/shard_map/ppermute | solution.py:23
  34.8 12.2 %copy-start.5 = (s32[32]{0:T(128)S(1)}, s32[32]{0:T(128)}, u32[]{:S(2)}) copy-start(s32[32]{0:T(128)} %param.13) | copy-start | bytes 388
  34.8 25.0 %all-to-all-start.1 = ((bf16[4,128,768]{2,1,0:T(8,128)(2,1)}), bf16[4,128,768]{2,1,0:T(8,128)(2,1)S(1)}, u32[]{:S(2)}, u32[]{:S(2)}) async-start(bf16[4,128,768]{2,1,0:T(8,128)(2,1)} %broadcast_in_dim.25), calls=%async_computation.1 | async-start | bytes 1572864 | tf_op jit(solution)/shard_map/all_to_all | solution.py:27
  43.8 9.5 %collective-permute-start.1 = (bf16[2,256,128]{2,1,0:T(8,128)(2,1)S(1)}, bf16[2,256,128]{2,1,0:T(8,128)(2,1)S(1)}, u32[]{:S(2)}, u32[]{:S(2)}) collective-permute-start(bf16[2,256,128]{2,1,0:T(8,128)(2,1)S(1)} %pad_maximum_fusion.1), channel_id=1, source_target_pairs={{0,8},{1,9},{2,10},{3,11},{4,12},{5,13},{6,14},{7,15},{8,0},{9,1},... | collective-permute-start | bytes 393224 | tf_op jit(solution)/shard_map/ppermute | solution.py:23
  53.3 9.3 %collective-permute-start.2 = (bf16[4,256,128]{2,1,0:T(8,128)(2,1)S(1)}, bf16[4,256,128]{2,1,0:T(8,128)(2,1)S(1)}, u32[]{:S(2)}, u32[]{:S(2)}) collective-permute-start(bf16[4,256,128]{2,1,0:T(8,128)(2,1)S(1)} %pad_maximum_fusion), channel_id=1, source_target_pairs={{0,4},{1,5},{2,6},{3,7},{4,0},{5,1},{6,2},{7,3},{8,12},{9,13},{10,... | collective-permute-start | bytes 786440 | tf_op jit(solution)/shard_map/ppermute | solution.py:23
  57.9 35.2 %collective-permute-start.7 = (bf16[4,128,768]{2,1,0:T(8,128)(2,1)S(1)}, bf16[4,128,768]{2,1,0:T(8,128)(2,1)S(1)}, u32[]{:S(2)}, u32[]{:S(2)}) collective-permute-start(bf16[4,128,768]{2,1,0:T(8,128)(2,1)S(1)} %all-to-all-done.w0), channel_id=1, source_target_pairs={{0,32},{32,0},{64,96},{96,64},{128,160},{160,128},{192,224},{224,1... | collective-permute-start | bytes 2359304 | tf_op jit(solution)/shard_map/ppermute | solution.py:23
  59.8 33.2 %collective-permute-start.8 = (bf16[4,128,768]{2,1,0:T(8,128)(2,1)S(1)}, bf16[4,128,768]{2,1,0:T(8,128)(2,1)S(1)}, u32[]{:S(2)}, u32[]{:S(2)}) collective-permute-start(bf16[4,128,768]{2,1,0:T(8,128)(2,1)S(1)} %all-to-all-done.1.w1), channel_id=1, source_target_pairs={{0,32},{32,0},{64,96},{96,64},{128,160},{160,128},{192,224},{224,1... | collective-permute-start | bytes 2359304 | tf_op jit(solution)/shard_map/ppermute | solution.py:23
  62.6 27.9 %collective-permute-start.5 = (bf16[8,256,128]{2,1,0:T(8,128)(2,1)S(1)}, bf16[8,256,128]{2,1,0:T(8,128)(2,1)S(1)}, u32[]{:S(2)}, u32[]{:S(2)}) collective-permute-start(bf16[8,256,128]{2,1,0:T(8,128)(2,1)S(1)} %constant_dynamic-update-slice_fusion.x0), channel_id=1, source_target_pairs={{0,3},{1,2},{2,1},{3,0},{4,7},{5,6},{6,5},{7,4},{8,11},{9,10},{10,... | collective-permute-start | bytes 1572872 | tf_op jit(solution)/shard_map/ppermute | solution.py:23
  67.3 23.2 %collective-permute-start.4 = (bf16[8,256,128]{2,1,0:T(8,128)(2,1)S(1)}, bf16[8,256,128]{2,1,0:T(8,128)(2,1)S(1)}, u32[]{:S(2)}, u32[]{:S(2)}) collective-permute-start(bf16[8,256,128]{2,1,0:T(8,128)(2,1)S(1)} %constant_dynamic-update-slice_fusion.x0), channel_id=1, source_target_pairs={{0,2},{1,3},{2,0},{3,1},{4,6},{5,7},{6,4},{7,5},{8,10},{9,11},{10,... | collective-permute-start | bytes 1572872 | tf_op jit(solution)/shard_map/ppermute | solution.py:23
  70.0 23.0 %collective-permute-start.3 = (bf16[8,256,128]{2,1,0:T(8,128)(2,1)S(1)}, bf16[8,256,128]{2,1,0:T(8,128)(2,1)S(1)}, u32[]{:S(2)}, u32[]{:S(2)}) collective-permute-start(bf16[8,256,128]{2,1,0:T(8,128)(2,1)S(1)} %constant_dynamic-update-slice_fusion.x0), channel_id=1, source_target_pairs={{0,1},{1,0},{2,3},{3,2},{4,5},{5,4},{6,7},{7,6},{8,9},{9,8},{10,11... | collective-permute-start | bytes 1572872 | tf_op jit(solution)/shard_map/ppermute | solution.py:23
  97.3 29.5 %collective-permute-start.16 = (bf16[4,128,768]{2,1,0:T(8,128)(2,1)S(1)}, bf16[4,128,768]{2,1,0:T(8,128)(2,1)S(1)}, u32[]{:S(2)}, u32[]{:S(2)}) collective-permute-start(bf16[4,128,768]{2,1,0:T(8,128)(2,1)S(1)} %get-tuple-element.27), channel_id=1, source_target_pairs={{0,32},{32,0},{64,96},{96,64},{128,160},{160,128},{192,224},{224,1... | collective-permute-start | bytes 2359304 | tf_op jit(solution)/shard_map/ppermute | solution.py:23
  100.6 12.4 %collective-permute-start.9 = (bf16[8,128,128]{2,1,0:T(8,128)(2,1)S(1)}, bf16[8,128,128]{2,1,0:T(8,128)(2,1)S(1)}, u32[]{:S(2)}, u32[]{:S(2)}) collective-permute-start(bf16[8,128,128]{2,1,0:T(8,128)(2,1)S(1)} %get-tuple-element.21), channel_id=1, source_target_pairs={{0,1},{1,0},{2,3},{3,2},{4,5},{5,4},{6,7},{7,6},{8,9},{9,8},{10,11... | collective-permute-start | bytes 786440 | tf_op jit(solution)/shard_map/ppermute | solution.py:23
  104.0 15.1 %collective-permute-start.10 = (bf16[8,128,128]{2,1,0:T(8,128)(2,1)S(1)}, bf16[8,128,128]{2,1,0:T(8,128)(2,1)S(1)}, u32[]{:S(2)}, u32[]{:S(2)}) collective-permute-start(bf16[8,128,128]{2,1,0:T(8,128)(2,1)S(1)} %get-tuple-element.22), channel_id=1, source_target_pairs={{0,2},{1,3},{2,0},{3,1},{4,6},{5,7},{6,4},{7,5},{8,10},{9,11},{10,... | collective-permute-start | bytes 786440 | tf_op jit(solution)/shard_map/ppermute | solution.py:23
  108.7 16.0 %collective-permute-start.11 = (bf16[8,128,128]{2,1,0:T(8,128)(2,1)S(1)}, bf16[8,128,128]{2,1,0:T(8,128)(2,1)S(1)}, u32[]{:S(2)}, u32[]{:S(2)}) collective-permute-start(bf16[8,128,128]{2,1,0:T(8,128)(2,1)S(1)} %get-tuple-element.23), channel_id=1, source_target_pairs={{0,3},{1,2},{2,1},{3,0},{4,7},{5,6},{6,5},{7,4},{8,11},{9,10},{10,... | collective-permute-start | bytes 786440 | tf_op jit(solution)/shard_map/ppermute | solution.py:23
  111.0 38.3 %collective-permute-start.15 = (bf16[4,128,768]{2,1,0:T(8,128)(2,1)}, bf16[4,128,768]{2,1,0:T(8,128)(2,1)S(1)}, u32[]{:S(2)}, u32[]{:S(2)}) collective-permute-start(bf16[4,128,768]{2,1,0:T(8,128)(2,1)} %get-tuple-element.25), channel_id=1, source_target_pairs={{0,32},{32,0},{64,96},{96,64},{128,160},{160,128},{192,224},{224,1... | collective-permute-start | bytes 2359304 | tf_op jit(solution)/shard_map/ppermute | solution.py:23
  124.8 7.9 %collective-permute-start.12 = (bf16[4,128,128]{2,1,0:T(8,128)(2,1)S(1)}, bf16[4,128,128]{2,1,0:T(8,128)(2,1)S(1)}, u32[]{:S(2)}, u32[]{:S(2)}) collective-permute-start(bf16[4,128,128]{2,1,0:T(8,128)(2,1)S(1)} %slice.78), channel_id=1, source_target_pairs={{0,4},{1,5},{2,6},{3,7},{4,0},{5,1},{6,2},{7,3},{8,12},{9,13},{10,... | collective-permute-start | bytes 393224 | tf_op jit(solution)/shard_map/ppermute | solution.py:23
  127.9 22.6 %all-to-all-start.3 = ((bf16[4,128,768]{2,1,0:T(8,128)(2,1)}), bf16[4,128,768]{2,1,0:T(8,128)(2,1)S(1)}, u32[]{:S(2)}, u32[]{:S(2)}) async-start(bf16[4,128,768]{2,1,0:T(8,128)(2,1)} %add_convert_fusion), calls=%async_computation.3 | async-start | bytes 1572864 | tf_op jit(solution)/shard_map/all_to_all | solution.py:27
  132.7 9.4 %collective-permute-start.13 = (bf16[2,128,128]{2,1,0:T(8,128)(2,1)S(1)}, bf16[2,128,128]{2,1,0:T(8,128)(2,1)S(1)}, u32[]{:S(2)}, u32[]{:S(2)}) collective-permute-start(bf16[2,128,128]{2,1,0:T(8,128)(2,1)S(1)} %slice.79), channel_id=1, source_target_pairs={{0,8},{1,9},{2,10},{3,11},{4,12},{5,13},{6,14},{7,15},{8,0},{9,1},... | collective-permute-start | bytes 196616 | tf_op jit(solution)/shard_map/ppermute | solution.py:23
  142.1 13.1 %collective-permute-start.14 = (bf16[1,128,128]{2,1,0:T(8,128)(2,1)S(1)}, bf16[1,128,128]{2,1,0:T(8,128)(2,1)S(1)}, u32[]{:S(2)}, u32[]{:S(2)}) collective-permute-start(bf16[1,128,128]{2,1,0:T(8,128)(2,1)S(1)} %slice.80), channel_id=1, source_target_pairs={{0,16},{1,17},{2,18},{3,19},{4,20},{5,21},{6,22},{7,23},{8,24},{9,... | collective-permute-start | bytes 98312 | tf_op jit(solution)/shard_map/ppermute | solution.py:23
  150.4 15.0 %all-to-all-start.2 = ((bf16[4,128,768]{2,1,0:T(8,128)(2,1)}), bf16[4,128,768]{2,1,0:T(8,128)(2,1)S(1)}, u32[]{:S(2)}, u32[]{:S(2)}) async-start(bf16[4,128,768]{2,1,0:T(8,128)(2,1)} %add_convert_fusion.1), calls=%async_computation.2 | async-start | bytes 1572864 | tf_op jit(solution)/shard_map/all_to_all | solution.py:27
  155.5 27.3 %collective-permute-start.17 = (bf16[128,768]{1,0:T(8,128)(2,1)S(1)}, bf16[128,768]{1,0:T(8,128)(2,1)S(1)}, u32[]{:S(2)}, u32[]{:S(2)}) collective-permute-start(bf16[128,768]{1,0:T(8,128)(2,1)S(1)} %reduce_sum.32), channel_id=1, source_target_pairs={{0,64},{32,96},{64,0},{96,32},{128,192},{160,224},{192,128},{224,1... | collective-permute-start | bytes 589832 | tf_op jit(solution)/shard_map/ppermute | solution.py:23

commit v2 on v1

--- a/solution.py
+++ b/solution.py
@@ -10,7 +10,7 @@
 LANES = 128
 BLK = 256
 Y_GROUPS = [[4 * y + r for y in range(4)] for r in range(4)]
-Z_OFFSETS = (0, 4, 2, 6, 1, 5, 3, 7)
+Z_OFFSETS = (0, 4, 2, 6)
 
 
 VMEM = pl.BlockSpec(memory_space=pltpu.VMEM)
@@ -39,13 +39,14 @@
     return (lax.broadcasted_iota(jnp.int32, shape, 1) < LANES // 2) == (parity == 0)
 
 
-def forward_kernel(place, keep_ref, x0, x1, x2, x3, w0, w1, w2, w3,
+def forward_kernel(place, keep_ref, lo0, lo1, lo2, lo3, hi0, hi1, hi2, hi3, w0, w1, w2, w3,
                    own0, own1, away0, away1, dgu, tok, cot, hid):
     side, core, parity, quarter = place[0], place[1], place[2], place[3]
     mask = halves_mask((TOK, LANES), parity)
-    for half, (even, odd) in enumerate(((x0, x1), (x2, x3))):
+    pairs = ((lo0, lo1, 0, 0), (lo2, lo3, 1, 0), (hi0, hi1, 0, 1), (hi2, hi3, 1, 1))
+    for even, odd, half, turn in pairs:
+        chunk = (half ^ core) * 2 + (turn ^ side)
         for s, a in enumerate(Z_OFFSETS):
-            chunk = (half ^ core) * 2 + (a % 2 ^ side)
             lanes = pl.ds(pl.multiple_of((chunk * 4 + (quarter ^ a // 2)) * LANES, LANES), LANES)
             e, f = even[s], odd[s]
             tok[:, lanes] = jnp.where(mask, e, f)
@@ -144,16 +145,17 @@
     w_own = gather(shard, "cand", Y_GROUPS)
     pieces = jnp.concatenate([pieces, swap(pieces, "hid", 8)], axis=0)
     pieces, place, keep = lax.optimization_barrier((pieces, place, keep))
-    pieces = jnp.concatenate([pieces, swap(pieces, "hid", 4)], axis=0)
-    xs = [pieces] + [swap(pieces, "hid", b) for b in (1, 2, 3)]
+    others = swap(pieces, "hid", 4)
+    los = [pieces] + [swap(pieces, "hid", b) for b in (1, 2, 3)]
+    his = [others] + [swap(others, "hid", b) for b in (1, 2, 3)]
     w_far = gather(far, "cand", Y_GROUPS)
     weights = [w_own, w_far, swap(w_own, "cand", 1), swap(w_far, "cand", 1)]
 
     grad = sds(4, 128, 3 * BLK)
     own0, own1, away0, away1, dgu = call(
-        forward_kernel, [grad] * 4 + [sds(TOK, 2 * BLK)], 2, 8,
+        forward_kernel, [grad] * 4 + [sds(TOK, 2 * BLK)], 2, 12,
         [pltpu.VMEM((TOK, 2048), BF16)] * 2 + [pltpu.VMEM((TOK, BLK), BF16)], 12,
-    )(place, keep, *xs, *weights)
+    )(place, keep, *los, *his, *weights)
     r0, *rs = call(token_grads_kernel, [sds(8, 128, 128)] * 4, 1, 5, [], 8)(place, dgu, *weights)
 
     both1 = own1.astype(F32) + swap(away1, "cand", 1).astype(F32)
@@ -164,12 +166,14 @@
     last = swap(total1.astype(BF16), "cand", 2)
     grads = lax.optimization_barrier(grads) + last.astype(F32)
 
+    arrived = [swap(r, "hid", b) for b, r in zip((1, 2, 3), rs)]
     part = r0.astype(F32)
-    for b, r in zip((1, 2, 3), rs):
-        part = part + swap(r, "hid", b).astype(F32)
+    for r in arrived:
+        part = part + r.astype(F32)
     for dist in (1, 2, 4):
         n = part.shape[0] // 2
-        part = part[:n] + swap(part[n:].astype(BF16), "hid", 4 * dist).astype(F32)
+        r = swap(part[n:].astype(BF16), "hid", 4 * dist)
+        part = part[:n] + r.astype(F32)
     part = part[0]
     left, right = part[:, :64], part[:, 64:]
     top, low = jnp.where(parity == 0, left, right), jnp.where(parity == 0, right, left)

time: 185 us -> 201 us (1.086)
  the two profiles are of different devices: /device:TPU:104 before, /device:TPU:8 now
where the time goes in v2:
time: 201 us; the launch traced here: 200 us
  starting transfers between devices  123 us (61%)
  waiting for transfers between devices  57.3 us (29%)
  local copies, waits for them, and re-layouts  8.53 us (4%)
  Pallas kernels  5.69 us (3%)
  other arithmetic  3.6 us (2%)
  between operations  2.36 us (1%)
    ppermute x21, starting transfers between devices, swap(): lax.ppermute(v, axis, [(k, k ^ offset) for k in range(lax.axis_size(axis))])  98.6 us
    ppermute x21, waiting for transfers between devices, swap(): lax.ppermute(v, axis, [(k, k ^ offset) for k in range(lax.axis_size(axis))])  57.3 us
    all_to_all x4, starting transfers between devices, exchange(): return lax.all_to_all(v, axis, 0, 0, axis_index_groups=groups, tiled=True)  23.9 us
    unnamed x20, local copies, waits for them, and re-layouts  5.85 us
    pallas_call x1, Pallas kernels, step(): call(forward_kernel, [grad] * 4 + [sds(TOK, 2 * BLK)], 2, 12, [pltpu.VMEM...  4.22 us
  transfers between devices with their start and end apart: 25, of which 11 were waited for; matrix products, arithmetic and copies ran while one was open for 2% of the time, Pallas kernels for 1%

profile of v2, /device:TPU:8, one launch (start us, length us, event | category | flops | bytes accessed | tf_op | source)
XLA Modules:
  0.0 200.0 jit_solution(12486471989558662859)
XLA Ops:
  0.6 0.8 copy-done.2
  1.5 0.8 copy-done.3
  2.3 0.8 copy-done.4
  3.2 1.0 broadcast_in_dim.24
  4.2 9.4 %all-to-all-start = ((bf16[4,128,768]{2,1,0:T(8,128)(2,1)}), bf16[4,128,768]{2,1,0:T(8,128)(2,1)S(1)}, u32[]{:S(2)}, u32[]{:S(2)}) async-start(bf16[4,128,768]{2,1,0:T(8,128)(2,1)} %broadcast_in_dim.24), calls=%async_computation | async-start | bytes 1572864 | tf_op jit(solution)/shard_map/all_to_all | solution.py:27
  13.6 11.4 %collective-permute-start.9 = (bf16[128,768]{1,0:T(8,128)(2,1)S(1)}, bf16[128,768]{1,0:T(8,128)(2,1)S(1)}, u32[]{:S(2)}, u32[]{:S(2)}) collective-permute-start(bf16[128,768]{1,0:T(8,128)(2,1)S(1)} %shard_map.102), channel_id=1, source_target_pairs={{0,64},{32,96},{64,0},{96,32},{128,192},{160,224},{192,128},{224,1... | collective-permute-start | bytes 589832 | tf_op jit(solution)/shard_map/ppermute | solution.py:23
  25.2 4.9 %collective-permute-done.9 = bf16[128,768]{1,0:T(8,128)(2,1)S(1)} collective-permute-done((bf16[128,768]{1,0:T(8,128)(2,1)S(1)}, bf16[128,768]{1,0:T(8,128)(2,1)S(1)}, u32[]{:S(2)}, u32[]{:S(2)}) %collective-permute-start.9) | collective-permute-done | bytes 196640 | tf_op jit(solution)/shard_map/ppermute | solution.py:23
  30.1 1.0 broadcast_in_dim.25
  31.1 4.9 %all-to-all-start.1 = ((bf16[4,128,768]{2,1,0:T(8,128)(2,1)}), bf16[4,128,768]{2,1,0:T(8,128)(2,1)S(1)}, u32[]{:S(2)}, u32[]{:S(2)}) async-start(bf16[4,128,768]{2,1,0:T(8,128)(2,1)} %broadcast_in_dim.25), calls=%async_computation.1 | async-start | bytes 1572864 | tf_op jit(solution)/shard_map/all_to_all | solution.py:27
  36.1 14.6 %collective-permute-start = (bf16[1,256,128]{2,1,0:T(8,128)(2,1)S(1)}, bf16[1,256,128]{2,1,0:T(8,128)(2,1)S(1)}, u32[]{:S(2)}, u32[]{:S(2)}) collective-permute-start(bf16[1,256,128]{2,1,0:T(8,128)(2,1)S(1)} %maximum_bitcast_fusion.2), channel_id=1, source_target_pairs={{0,16},{1,17},{2,18},{3,19},{4,20},{5,21},{6,22},{7,23},{8,24},{9,... | collective-permute-start | bytes 196616 | tf_op jit(solution)/shard_map/ppermute | solution.py:23
  50.8 2.2 %collective-permute-done = bf16[1,256,128]{2,1,0:T(8,128)(2,1)S(1)} collective-permute-done((bf16[1,256,128]{2,1,0:T(8,128)(2,1)S(1)}, bf16[1,256,128]{2,1,0:T(8,128)(2,1)S(1)}, u32[]{:S(2)}, u32[]{:S(2)}) %collective-permute-start) | collective-permute-done | bytes 65568 | tf_op jit(solution)/shard_map/ppermute | solution.py:23
  53.0 8.3 %collective-permute-start.1 = (bf16[2,256,128]{2,1,0:T(8,128)(2,1)S(1)}, bf16[2,256,128]{2,1,0:T(8,128)(2,1)S(1)}, u32[]{:S(2)}, u32[]{:S(2)}) collective-permute-start(bf16[2,256,128]{2,1,0:T(8,128)(2,1)S(1)} %pad_maximum_fusion.1), channel_id=1, source_target_pairs={{0,8},{1,9},{2,10},{3,11},{4,12},{5,13},{6,14},{7,15},{8,0},{9,1},... | collective-permute-start | bytes 393224 | tf_op jit(solution)/shard_map/ppermute | solution.py:23
  63.4 2.3 %collective-permute-done.1 = bf16[2,256,128]{2,1,0:T(8,128)(2,1)S(1)} collective-permute-done((bf16[2,256,128]{2,1,0:T(8,128)(2,1)S(1)}, bf16[2,256,128]{2,1,0:T(8,128)(2,1)S(1)}, u32[]{:S(2)}, u32[]{:S(2)}) %collective-permute-start.1) | collective-permute-done | bytes 131104 | tf_op jit(solution)/shard_map/ppermute | solution.py:23
  65.7 1.9 collective-permute-start.5
  67.6 1.9 collective-permute-start.10
  69.6 2.4 %collective-permute-start.11 = (bf16[4,128,768]{2,1,0:T(8,128)(2,1)S(1)}, bf16[4,128,768]{2,1,0:T(8,128)(2,1)S(1)}, u32[]{:S(2)}, u32[]{:S(2)}) collective-permute-start(bf16[4,128,768]{2,1,0:T(8,128)(2,1)S(1)} %all-to-all-done.1.w1), channel_id=1, source_target_pairs={{0,32},{32,0},{64,96},{96,64},{128,160},{160,128},{192,224},{224,1... | collective-permute-start | bytes 2359304 | tf_op jit(solution)/shard_map/ppermute | solution.py:23
  72.0 4.7 %collective-permute-start.4 = (bf16[4,256,128]{2,1,0:T(8,128)(2,1)S(1)}, bf16[4,256,128]{2,1,0:T(8,128)(2,1)S(1)}, u32[]{:S(2)}, u32[]{:S(2)}) collective-permute-start(bf16[4,256,128]{2,1,0:T(8,128)(2,1)S(1)} %pad_maximum_fusion.lo0), channel_id=1, source_target_pairs={{0,3},{1,2},{2,1},{3,0},{4,7},{5,6},{6,5},{7,4},{8,11},{9,10},{10,... | collective-permute-start | bytes 786440 | tf_op jit(solution)/shard_map/ppermute | solution.py:23
  76.7 2.7 %collective-permute-start.3 = (bf16[4,256,128]{2,1,0:T(8,128)(2,1)S(1)}, bf16[4,256,128]{2,1,0:T(8,128)(2,1)S(1)}, u32[]{:S(2)}, u32[]{:S(2)}) collective-permute-start(bf16[4,256,128]{2,1,0:T(8,128)(2,1)S(1)} %pad_maximum_fusion.lo0), channel_id=1, source_target_pairs={{0,2},{1,3},{2,0},{3,1},{4,6},{5,7},{6,4},{7,5},{8,10},{9,11},{10,... | collective-permute-start | bytes 786440 | tf_op jit(solution)/shard_map/ppermute | solution.py:23
  79.4 2.4 %collective-permute-start.2 = (bf16[4,256,128]{2,1,0:T(8,128)(2,1)S(1)}, bf16[4,256,128]{2,1,0:T(8,128)(2,1)S(1)}, u32[]{:S(2)}, u32[]{:S(2)}) collective-permute-start(bf16[4,256,128]{2,1,0:T(8,128)(2,1)S(1)} %pad_maximum_fusion.lo0), channel_id=1, source_target_pairs={{0,1},{1,0},{2,3},{3,2},{4,5},{5,4},{6,7},{7,6},{8,9},{9,8},{10,11... | collective-permute-start | bytes 786440 | tf_op jit(solution)/shard_map/ppermute | solution.py:23
  81.8 6.8 %collective-permute-done.4.lo3 = bf16[4,256,128]{2,1,0:T(8,128)(2,1)S(1)} collective-permute-done((bf16[4,256,128]{2,1,0:T(8,128)(2,1)S(1)}, bf16[4,256,128]{2,1,0:T(8,128)(2,1)S(1)}, u32[]{:S(2)}, u32[]{:S(2)}) %collective-permute-start.4) | collective-permute-done | bytes 262176 | tf_op jit(solution)/shard_map/ppermute | solution.py:23
  88.6 5.0 %collective-permute-start.8 = (bf16[4,256,128]{2,1,0:T(8,128)(2,1)S(1)}, bf16[4,256,128]{2,1,0:T(8,128)(2,1)S(1)}, u32[]{:S(2)}, u32[]{:S(2)}) collective-permute-start(bf16[4,256,128]{2,1,0:T(8,128)(2,1)S(1)} %collective-permute-done.5.hi0), channel_id=1, source_target_pairs={{0,3},{1,2},{2,1},{3,0},{4,7},{5,6},{6,5},{7,4},{8,11},{9,10},{10,... | collective-permute-start | bytes 786440 | tf_op jit(solution)/shard_map/ppermute | solution.py:23
  93.6 1.9 collective-permute-start.7
  95.5 2.9 %collective-permute-start.6 = (bf16[4,256,128]{2,1,0:T(8,128)(2,1)S(1)}, bf16[4,256,128]{2,1,0:T(8,128)(2,1)S(1)}, u32[]{:S(2)}, u32[]{:S(2)}) collective-permute-start(bf16[4,256,128]{2,1,0:T(8,128)(2,1)S(1)} %collective-permute-done.5.hi0), channel_id=1, source_target_pairs={{0,1},{1,0},{2,3},{3,2},{4,5},{5,4},{6,7},{7,6},{8,9},{9,8},{10,11... | collective-permute-start | bytes 786440 | tf_op jit(solution)/shard_map/ppermute | solution.py:23
  99.2 4.9 %collective-permute-done.8.hi3 = bf16[4,256,128]{2,1,0:T(8,128)(2,1)S(1)} collective-permute-done((bf16[4,256,128]{2,1,0:T(8,128)(2,1)S(1)}, bf16[4,256,128]{2,1,0:T(8,128)(2,1)S(1)}, u32[]{:S(2)}, u32[]{:S(2)}) %collective-permute-start.8) | collective-permute-done | bytes 262176 | tf_op jit(solution)/shard_map/ppermute | solution.py:23
  104.1 2.1 %collective-permute-done.7.hi2 = bf16[4,256,128]{2,1,0:T(8,128)(2,1)S(1)} collective-permute-done((bf16[4,256,128]{2,1,0:T(8,128)(2,1)S(1)}, bf16[4,256,128]{2,1,0:T(8,128)(2,1)S(1)}, u32[]{:S(2)}, u32[]{:S(2)}) %collective-permute-start.7) | collective-permute-done | bytes 262176 | tf_op jit(solution)/shard_map/ppermute | solution.py:23
  106.2 1.2 collective-permute-done.6.hi1
  107.4 0.9 copy-done.1
  108.3 4.2 %shard_map.103 = (bf16[4,128,768]{2,1,0:T(8,128)(2,1)S(1)}, bf16[4,128,768]{2,1,0:T(8,128)(2,1)S(1)}, bf16[4,128,768]{2,1,0:T(8,128)(2,1)}, bf16[4,128,768]{2,1,0:T(8,128)(2,1)S(1)}, bf16[256,512]{1,0:T(8,128)(2,1)S(1)}) custom-call(s32[4]{0:T(128)S(1)} %pad_add_fusion.place, f32[1]{0:T(128)} %bitcast.8.keep_ref, ...), custom_call_target="tpu_custom_call" | custom-call | tf_op jit(solution)/shard_map/pallas_call | solution.py:155
  112.6 1.9 collective-permute-start.19
  114.5 1.4 shard_map.104
  115.9 3.1 %collective-permute-start.12 = (bf16[8,128,128]{2,1,0:T(8,128)(2,1)S(1)}, bf16[8,128,128]{2,1,0:T(8,128)(2,1)S(1)}, u32[]{:S(2)}, u32[]{:S(2)}) collective-permute-start(bf16[8,128,128]{2,1,0:T(8,128)(2,1)S(1)} %get-tuple-element.21), channel_id=1, source_target_pairs={{0,1},{1,0},{2,3},{3,2},{4,5},{5,4},{6,7},{7,6},{8,9},{9,8},{10,11... | collective-permute-start | bytes 786440 | tf_op jit(solution)/shard_map/ppermute | solution.py:23
  119.0 5.1 %collective-permute-start.13 = (bf16[8,128,128]{2,1,0:T(8,128)(2,1)S(1)}, bf16[8,128,128]{2,1,0:T(8,128)(2,1)S(1)}, u32[]{:S(2)}, u32[]{:S(2)}) collective-permute-start(bf16[8,128,128]{2,1,0:T(8,128)(2,1)S(1)} %get-tuple-element.22), channel_id=1, source_target_pairs={{0,2},{1,3},{2,0},{3,1},{4,6},{5,7},{6,4},{7,5},{8,10},{9,11},{10,... | collective-permute-start | bytes 786440 | tf_op jit(solution)/shard_map/ppermute | solution.py:23
  124.1 2.2 %collective-permute-start.14 = (bf16[8,128,128]{2,1,0:T(8,128)(2,1)S(1)}, bf16[8,128,128]{2,1,0:T(8,128)(2,1)S(1)}, u32[]{:S(2)}, u32[]{:S(2)}) collective-permute-start(bf16[8,128,128]{2,1,0:T(8,128)(2,1)S(1)} %get-tuple-element.23), channel_id=1, source_target_pairs={{0,3},{1,2},{2,1},{3,0},{4,7},{5,6},{6,5},{7,4},{8,11},{9,10},{10,... | collective-permute-start | bytes 786440 | tf_op jit(solution)/shard_map/ppermute | solution.py:23
  126.3 1.9 collective-permute-start.18
  128.3 6.3 %collective-permute-done.13 = bf16[8,128,128]{2,1,0:T(8,128)(2,1)S(1)} collective-permute-done((bf16[8,128,128]{2,1,0:T(8,128)(2,1)S(1)}, bf16[8,128,128]{2,1,0:T(8,128)(2,1)S(1)}, u32[]{:S(2)}, u32[]{:S(2)}) %collective-permute-start.13) | collective-permute-done | bytes 262176 | tf_op jit(solution)/shard_map/ppermute | solution.py:23
  134.6 5.5 %collective-permute-done.14 = bf16[8,128,128]{2,1,0:T(8,128)(2,1)S(1)} collective-permute-done((bf16[8,128,128]{2,1,0:T(8,128)(2,1)S(1)}, bf16[8,128,128]{2,1,0:T(8,128)(2,1)S(1)}, u32[]{:S(2)}, u32[]{:S(2)}) %collective-permute-start.14) | collective-permute-done | bytes 262176 | tf_op jit(solution)/shard_map/ppermute | solution.py:23
  140.3 3.9 %collective-permute-start.15 = (bf16[4,128,128]{2,1,0:T(8,128)(2,1)S(1)}, bf16[4,128,128]{2,1,0:T(8,128)(2,1)S(1)}, u32[]{:S(2)}, u32[]{:S(2)}) collective-permute-start(bf16[4,128,128]{2,1,0:T(8,128)(2,1)S(1)} %slice.78), channel_id=1, source_target_pairs={{0,4},{1,5},{2,6},{3,7},{4,0},{5,1},{6,2},{7,3},{8,12},{9,13},{10,... | collective-permute-start | bytes 393224 | tf_op jit(solution)/shard_map/ppermute | solution.py:23
  144.2 1.1 add_convert_fusion
  145.3 4.8 %all-to-all-start.3 = ((bf16[4,128,768]{2,1,0:T(8,128)(2,1)}), bf16[4,128,768]{2,1,0:T(8,128)(2,1)S(1)}, u32[]{:S(2)}, u32[]{:S(2)}) async-start(bf16[4,128,768]{2,1,0:T(8,128)(2,1)} %add_convert_fusion), calls=%async_computation.3 | async-start | bytes 1572864 | tf_op jit(solution)/shard_map/all_to_all | solution.py:27
  150.2 3.4 %collective-permute-start.16 = (bf16[2,128,128]{2,1,0:T(8,128)(2,1)S(1)}, bf16[2,128,128]{2,1,0:T(8,128)(2,1)S(1)}, u32[]{:S(2)}, u32[]{:S(2)}) collective-permute-start(bf16[2,128,128]{2,1,0:T(8,128)(2,1)S(1)} %slice.79), channel_id=1, source_target_pairs={{0,8},{1,9},{2,10},{3,11},{4,12},{5,13},{6,14},{7,15},{8,0},{9,1},... | collective-permute-start | bytes 196616 | tf_op jit(solution)/shard_map/ppermute | solution.py:23
  153.6 3.8 %collective-permute-done.16 = bf16[2,128,128]{2,1,0:T(8,128)(2,1)S(1)} collective-permute-done((bf16[2,128,128]{2,1,0:T(8,128)(2,1)S(1)}, bf16[2,128,128]{2,1,0:T(8,128)(2,1)S(1)}, u32[]{:S(2)}, u32[]{:S(2)}) %collective-permute-start.16) | collective-permute-done | bytes 65568 | tf_op jit(solution)/shard_map/ppermute | solution.py:23
  157.4 7.6 %collective-permute-start.17 = (bf16[1,128,128]{2,1,0:T(8,128)(2,1)S(1)}, bf16[1,128,128]{2,1,0:T(8,128)(2,1)S(1)}, u32[]{:S(2)}, u32[]{:S(2)}) collective-permute-start(bf16[1,128,128]{2,1,0:T(8,128)(2,1)S(1)} %slice.80), channel_id=1, source_target_pairs={{0,16},{1,17},{2,18},{3,19},{4,20},{5,21},{6,22},{7,23},{8,24},{9,... | collective-permute-start | bytes 98312 | tf_op jit(solution)/shard_map/ppermute | solution.py:23
  165.1 1.1 add_convert_fusion.1
  166.1 4.8 %all-to-all-start.2 = ((bf16[4,128,768]{2,1,0:T(8,128)(2,1)}), bf16[4,128,768]{2,1,0:T(8,128)(2,1)S(1)}, u32[]{:S(2)}, u32[]{:S(2)}) async-start(bf16[4,128,768]{2,1,0:T(8,128)(2,1)} %add_convert_fusion.1), calls=%async_computation.2 | async-start | bytes 1572864 | tf_op jit(solution)/shard_map/all_to_all | solution.py:27
  171.2 9.2 %collective-permute-start.20 = (bf16[128,768]{1,0:T(8,128)(2,1)S(1)}, bf16[128,768]{1,0:T(8,128)(2,1)S(1)}, u32[]{:S(2)}, u32[]{:S(2)}) collective-permute-start(bf16[128,768]{1,0:T(8,128)(2,1)S(1)} %reduce_sum.32), channel_id=1, source_target_pairs={{0,64},{32,96},{64,0},{96,32},{128,192},{160,224},{192,128},{224,1... | collective-permute-start | bytes 589832 | tf_op jit(solution)/shard_map/ppermute | solution.py:23
  181.3 17.2 %collective-permute-done.20 = bf16[128,768]{1,0:T(8,128)(2,1)S(1)} collective-permute-done((bf16[128,768]{1,0:T(8,128)(2,1)S(1)}, bf16[128,768]{1,0:T(8,128)(2,1)S(1)}, u32[]{:S(2)}, u32[]{:S(2)}) %collective-permute-start.20) | collective-permute-done | bytes 196640 | tf_op jit(solution)/shard_map/ppermute | solution.py:23
  198.5 0.7 fusion.3
  199.2 0.8 copy.23
  (50 shorter events, 3.2 us)
Async XLA Ops:
  0.6 0.8 copy-start.2
  1.5 0.8 copy-start.3
  2.3 0.8 copy-start.4
  4.2 20.8 %copy-start.5 = (bf16[1,256,64]{1,2,0:T(8,128)(2,1)S(1)}, bf16[1,256,64]{1,2,0:T(8,128)(2,1)}, u32[]{:S(2)}) copy-start(bf16[1,256,64]{1,2,0:T(8,128)(2,1)} %param.7) | copy-start | bytes 98308
  4.2 20.9 %copy-start.6 = (bf16[1,256,64]{1,2,0:T(8,128)(2,1)S(1)}, bf16[1,256,64]{1,2,0:T(8,128)(2,1)}, u32[]{:S(2)}) copy-start(bf16[1,256,64]{1,2,0:T(8,128)(2,1)} %param.8) | copy-start | bytes 98308
  4.2 26.0 %all-to-all-start = ((bf16[4,128,768]{2,1,0:T(8,128)(2,1)}), bf16[4,128,768]{2,1,0:T(8,128)(2,1)S(1)}, u32[]{:S(2)}, u32[]{:S(2)}) async-start(bf16[4,128,768]{2,1,0:T(8,128)(2,1)} %broadcast_in_dim.24), calls=%async_computation | async-start | bytes 1572864 | tf_op jit(solution)/shard_map/all_to_all | solution.py:27
  13.6 16.6 %collective-permute-start.9 = (bf16[128,768]{1,0:T(8,128)(2,1)S(1)}, bf16[128,768]{1,0:T(8,128)(2,1)S(1)}, u32[]{:S(2)}, u32[]{:S(2)}) collective-permute-start(bf16[128,768]{1,0:T(8,128)(2,1)S(1)} %shard_map.102), channel_id=1, source_target_pairs={{0,64},{32,96},{64,0},{96,32},{128,192},{160,224},{192,128},{224,1... | collective-permute-start | bytes 589832 | tf_op jit(solution)/shard_map/ppermute | solution.py:23
  31.1 30.2 %copy-start.7 = (s32[32]{0:T(128)S(1)}, s32[32]{0:T(128)}, u32[]{:S(2)}) copy-start(s32[32]{0:T(128)} %param.13) | copy-start | bytes 388
  31.1 38.5 %all-to-all-start.1 = ((bf16[4,128,768]{2,1,0:T(8,128)(2,1)}), bf16[4,128,768]{2,1,0:T(8,128)(2,1)S(1)}, u32[]{:S(2)}, u32[]{:S(2)}) async-start(bf16[4,128,768]{2,1,0:T(8,128)(2,1)} %broadcast_in_dim.25), calls=%async_computation.1 | async-start | bytes 1572864 | tf_op jit(solution)/shard_map/all_to_all | solution.py:27
  36.1 16.9 %collective-permute-start = (bf16[1,256,128]{2,1,0:T(8,128)(2,1)S(1)}, bf16[1,256,128]{2,1,0:T(8,128)(2,1)S(1)}, u32[]{:S(2)}, u32[]{:S(2)}) collective-permute-start(bf16[1,256,128]{2,1,0:T(8,128)(2,1)S(1)} %maximum_bitcast_fusion.2), channel_id=1, source_target_pairs={{0,16},{1,17},{2,18},{3,19},{4,20},{5,21},{6,22},{7,23},{8,24},{9,... | collective-permute-start | bytes 196616 | tf_op jit(solution)/shard_map/ppermute | solution.py:23
  53.0 12.7 %collective-permute-start.1 = (bf16[2,256,128]{2,1,0:T(8,128)(2,1)S(1)}, bf16[2,256,128]{2,1,0:T(8,128)(2,1)S(1)}, u32[]{:S(2)}, u32[]{:S(2)}) collective-permute-start(bf16[2,256,128]{2,1,0:T(8,128)(2,1)S(1)} %pad_maximum_fusion.1), channel_id=1, source_target_pairs={{0,8},{1,9},{2,10},{3,11},{4,12},{5,13},{6,14},{7,15},{8,0},{9,1},... | collective-permute-start | bytes 393224 | tf_op jit(solution)/shard_map/ppermute | solution.py:23
  65.7 13.7 %collective-permute-start.5 = (bf16[4,256,128]{2,1,0:T(8,128)(2,1)S(1)}, bf16[4,256,128]{2,1,0:T(8,128)(2,1)S(1)}, u32[]{:S(2)}, u32[]{:S(2)}) collective-permute-start(bf16[4,256,128]{2,1,0:T(8,128)(2,1)S(1)} %pad_maximum_fusion.lo0), channel_id=1, source_target_pairs={{0,4},{1,5},{2,6},{3,7},{4,0},{5,1},{6,2},{7,3},{8,12},{9,13},{10,... | collective-permute-start | bytes 786440 | tf_op jit(solution)/shard_map/ppermute | solution.py:23
  67.6 39.7 %collective-permute-start.10 = (bf16[4,128,768]{2,1,0:T(8,128)(2,1)S(1)}, bf16[4,128,768]{2,1,0:T(8,128)(2,1)S(1)}, u32[]{:S(2)}, u32[]{:S(2)}) collective-permute-start(bf16[4,128,768]{2,1,0:T(8,128)(2,1)S(1)} %all-to-all-done.w0), channel_id=1, source_target_pairs={{0,32},{32,0},{64,96},{96,64},{128,160},{160,128},{192,224},{224,1... | collective-permute-start | bytes 2359304 | tf_op jit(solution)/shard_map/ppermute | solution.py:23
  69.6 37.8 %collective-permute-start.11 = (bf16[4,128,768]{2,1,0:T(8,128)(2,1)S(1)}, bf16[4,128,768]{2,1,0:T(8,128)(2,1)S(1)}, u32[]{:S(2)}, u32[]{:S(2)}) collective-permute-start(bf16[4,128,768]{2,1,0:T(8,128)(2,1)S(1)} %all-to-all-done.1.w1), channel_id=1, source_target_pairs={{0,32},{32,0},{64,96},{96,64},{128,160},{160,128},{192,224},{224,1... | collective-permute-start | bytes 2359304 | tf_op jit(solution)/shard_map/ppermute | solution.py:23
  72.0 16.6 %collective-permute-start.4 = (bf16[4,256,128]{2,1,0:T(8,128)(2,1)S(1)}, bf16[4,256,128]{2,1,0:T(8,128)(2,1)S(1)}, u32[]{:S(2)}, u32[]{:S(2)}) collective-permute-start(bf16[4,256,128]{2,1,0:T(8,128)(2,1)S(1)} %pad_maximum_fusion.lo0), channel_id=1, source_target_pairs={{0,3},{1,2},{2,1},{3,0},{4,7},{5,6},{6,5},{7,4},{8,11},{9,10},{10,... | collective-permute-start | bytes 786440 | tf_op jit(solution)/shard_map/ppermute | solution.py:23
  76.7 16.9 %collective-permute-start.3 = (bf16[4,256,128]{2,1,0:T(8,128)(2,1)S(1)}, bf16[4,256,128]{2,1,0:T(8,128)(2,1)S(1)}, u32[]{:S(2)}, u32[]{:S(2)}) collective-permute-start(bf16[4,256,128]{2,1,0:T(8,128)(2,1)S(1)} %pad_maximum_fusion.lo0), channel_id=1, source_target_pairs={{0,2},{1,3},{2,0},{3,1},{4,6},{5,7},{6,4},{7,5},{8,10},{9,11},{10,... | collective-permute-start | bytes 786440 | tf_op jit(solution)/shard_map/ppermute | solution.py:23
  79.4 16.1 %collective-permute-start.2 = (bf16[4,256,128]{2,1,0:T(8,128)(2,1)S(1)}, bf16[4,256,128]{2,1,0:T(8,128)(2,1)S(1)}, u32[]{:S(2)}, u32[]{:S(2)}) collective-permute-start(bf16[4,256,128]{2,1,0:T(8,128)(2,1)S(1)} %pad_maximum_fusion.lo0), channel_id=1, source_target_pairs={{0,1},{1,0},{2,3},{3,2},{4,5},{5,4},{6,7},{7,6},{8,9},{9,8},{10,11... | collective-permute-start | bytes 786440 | tf_op jit(solution)/shard_map/ppermute | solution.py:23
  88.6 15.5 %collective-permute-start.8 = (bf16[4,256,128]{2,1,0:T(8,128)(2,1)S(1)}, bf16[4,256,128]{2,1,0:T(8,128)(2,1)S(1)}, u32[]{:S(2)}, u32[]{:S(2)}) collective-permute-start(bf16[4,256,128]{2,1,0:T(8,128)(2,1)S(1)} %collective-permute-done.5.hi0), channel_id=1, source_target_pairs={{0,3},{1,2},{2,1},{3,0},{4,7},{5,6},{6,5},{7,4},{8,11},{9,10},{10,... | collective-permute-start | bytes 786440 | tf_op jit(solution)/shard_map/ppermute | solution.py:23
  93.6 12.6 %collective-permute-start.7 = (bf16[4,256,128]{2,1,0:T(8,128)(2,1)S(1)}, bf16[4,256,128]{2,1,0:T(8,128)(2,1)S(1)}, u32[]{:S(2)}, u32[]{:S(2)}) collective-permute-start(bf16[4,256,128]{2,1,0:T(8,128)(2,1)S(1)} %collective-permute-done.5.hi0), channel_id=1, source_target_pairs={{0,2},{1,3},{2,0},{3,1},{4,6},{5,7},{6,4},{7,5},{8,10},{9,11},{10,... | collective-permute-start | bytes 786440 | tf_op jit(solution)/shard_map/ppermute | solution.py:23
  95.5 11.8 %collective-permute-start.6 = (bf16[4,256,128]{2,1,0:T(8,128)(2,1)S(1)}, bf16[4,256,128]{2,1,0:T(8,128)(2,1)S(1)}, u32[]{:S(2)}, u32[]{:S(2)}) collective-permute-start(bf16[4,256,128]{2,1,0:T(8,128)(2,1)S(1)} %collective-permute-done.5.hi0), channel_id=1, source_target_pairs={{0,1},{1,0},{2,3},{3,2},{4,5},{5,4},{6,7},{7,6},{8,9},{9,8},{10,11... | collective-permute-start | bytes 786440 | tf_op jit(solution)/shard_map/ppermute | solution.py:23
  98.5 0.7 copy-start
  107.4 1.0 copy-start.1
  112.6 31.6 %collective-permute-start.19 = (bf16[4,128,768]{2,1,0:T(8,128)(2,1)S(1)}, bf16[4,128,768]{2,1,0:T(8,128)(2,1)S(1)}, u32[]{:S(2)}, u32[]{:S(2)}) collective-permute-start(bf16[4,128,768]{2,1,0:T(8,128)(2,1)S(1)} %get-tuple-element.27), channel_id=1, source_target_pairs={{0,32},{32,0},{64,96},{96,64},{128,160},{160,128},{192,224},{224,1... | collective-permute-start | bytes 2359304 | tf_op jit(solution)/shard_map/ppermute | solution.py:23
  115.9 12.4 %collective-permute-start.12 = (bf16[8,128,128]{2,1,0:T(8,128)(2,1)S(1)}, bf16[8,128,128]{2,1,0:T(8,128)(2,1)S(1)}, u32[]{:S(2)}, u32[]{:S(2)}) collective-permute-start(bf16[8,128,128]{2,1,0:T(8,128)(2,1)S(1)} %get-tuple-element.21), channel_id=1, source_target_pairs={{0,1},{1,0},{2,3},{3,2},{4,5},{5,4},{6,7},{7,6},{8,9},{9,8},{10,11... | collective-permute-start | bytes 786440 | tf_op jit(solution)/shard_map/ppermute | solution.py:23
  119.0 15.6 %collective-permute-start.13 = (bf16[8,128,128]{2,1,0:T(8,128)(2,1)S(1)}, bf16[8,128,128]{2,1,0:T(8,128)(2,1)S(1)}, u32[]{:S(2)}, u32[]{:S(2)}) collective-permute-start(bf16[8,128,128]{2,1,0:T(8,128)(2,1)S(1)} %get-tuple-element.22), channel_id=1, source_target_pairs={{0,2},{1,3},{2,0},{3,1},{4,6},{5,7},{6,4},{7,5},{8,10},{9,11},{10,... | collective-permute-start | bytes 786440 | tf_op jit(solution)/shard_map/ppermute | solution.py:23
  124.1 16.0 %collective-permute-start.14 = (bf16[8,128,128]{2,1,0:T(8,128)(2,1)S(1)}, bf16[8,128,128]{2,1,0:T(8,128)(2,1)S(1)}, u32[]{:S(2)}, u32[]{:S(2)}) collective-permute-start(bf16[8,128,128]{2,1,0:T(8,128)(2,1)S(1)} %get-tuple-element.23), channel_id=1, source_target_pairs={{0,3},{1,2},{2,1},{3,0},{4,7},{5,6},{6,5},{7,4},{8,11},{9,10},{10,... | collective-permute-start | bytes 786440 | tf_op jit(solution)/shard_map/ppermute | solution.py:23
  126.3 38.7 %collective-permute-start.18 = (bf16[4,128,768]{2,1,0:T(8,128)(2,1)}, bf16[4,128,768]{2,1,0:T(8,128)(2,1)S(1)}, u32[]{:S(2)}, u32[]{:S(2)}) collective-permute-start(bf16[4,128,768]{2,1,0:T(8,128)(2,1)} %get-tuple-element.25), channel_id=1, source_target_pairs={{0,32},{32,0},{64,96},{96,64},{128,160},{160,128},{192,224},{224,1... | collective-permute-start | bytes 2359304 | tf_op jit(solution)/shard_map/ppermute | solution.py:23
  140.3 9.9 %collective-permute-start.15 = (bf16[4,128,128]{2,1,0:T(8,128)(2,1)S(1)}, bf16[4,128,128]{2,1,0:T(8,128)(2,1)S(1)}, u32[]{:S(2)}, u32[]{:S(2)}) collective-permute-start(bf16[4,128,128]{2,1,0:T(8,128)(2,1)S(1)} %slice.78), channel_id=1, source_target_pairs={{0,4},{1,5},{2,6},{3,7},{4,0},{5,1},{6,2},{7,3},{8,12},{9,13},{10,... | collective-permute-start | bytes 393224 | tf_op jit(solution)/shard_map/ppermute | solution.py:23
  145.3 20.8 %all-to-all-start.3 = ((bf16[4,128,768]{2,1,0:T(8,128)(2,1)}), bf16[4,128,768]{2,1,0:T(8,128)(2,1)S(1)}, u32[]{:S(2)}, u32[]{:S(2)}) async-start(bf16[4,128,768]{2,1,0:T(8,128)(2,1)} %add_convert_fusion), calls=%async_computation.3 | async-start | bytes 1572864 | tf_op jit(solution)/shard_map/all_to_all | solution.py:27
  150.2 7.2 %collective-permute-start.16 = (bf16[2,128,128]{2,1,0:T(8,128)(2,1)S(1)}, bf16[2,128,128]{2,1,0:T(8,128)(2,1)S(1)}, u32[]{:S(2)}, u32[]{:S(2)}) collective-permute-start(bf16[2,128,128]{2,1,0:T(8,128)(2,1)S(1)} %slice.79), channel_id=1, source_target_pairs={{0,8},{1,9},{2,10},{3,11},{4,12},{5,13},{6,14},{7,15},{8,0},{9,1},... | collective-permute-start | bytes 196616 | tf_op jit(solution)/shard_map/ppermute | solution.py:23
  157.4 13.5 %collective-permute-start.17 = (bf16[1,128,128]{2,1,0:T(8,128)(2,1)S(1)}, bf16[1,128,128]{2,1,0:T(8,128)(2,1)S(1)}, u32[]{:S(2)}, u32[]{:S(2)}) collective-permute-start(bf16[1,128,128]{2,1,0:T(8,128)(2,1)S(1)} %slice.80), channel_id=1, source_target_pairs={{0,16},{1,17},{2,18},{3,19},{4,20},{5,21},{6,22},{7,23},{8,24},{9,... | collective-permute-start | bytes 98312 | tf_op jit(solution)/shard_map/ppermute | solution.py:23
  166.1 15.0 %all-to-all-start.2 = ((bf16[4,128,768]{2,1,0:T(8,128)(2,1)}), bf16[4,128,768]{2,1,0:T(8,128)(2,1)S(1)}, u32[]{:S(2)}, u32[]{:S(2)}) async-start(bf16[4,128,768]{2,1,0:T(8,128)(2,1)} %add_convert_fusion.1), calls=%async_computation.2 | async-start | bytes 1572864 | tf_op jit(solution)/shard_map/all_to_all | solution.py:27
  171.2 27.3 %collective-permute-start.20 = (bf16[128,768]{1,0:T(8,128)(2,1)S(1)}, bf16[128,768]{1,0:T(8,128)(2,1)S(1)}, u32[]{:S(2)}, u32[]{:S(2)}) collective-permute-start(bf16[128,768]{1,0:T(8,128)(2,1)S(1)} %reduce_sum.32), channel_id=1, source_target_pairs={{0,64},{32,96},{64,0},{96,32},{128,192},{160,224},{192,128},{224,1... | collective-permute-start | bytes 589832 | tf_op jit(solution)/shard_map/ppermute | solution.py:23
